TPU v7x, 128 devices: a whole 4x4x4 slice. The times are simulated.
128 devices in a mesh: fsdp: 16 (over y_hi, z, core), tensor: 8 (over y_lo, x).
Axes of the slice: x: 4, y: 4 (y_hi: 2, y_lo: 2; y = y_hi * 2 + y_lo), z: 4, core: 2. Of those that a mesh axis runs over, the one named last changes fastest.
Arguments:
- states: bfloat16 [4096, 8192], P('fsdp'), may hold values from -64 to 64
- segment_ids: int32 [16, 256], P('fsdp'), may hold values from 0 to 3, never falling along the last dimension, each value on 1 to 128 neighbouring positions
- attn_gain: float32 [8192], replicated, may hold values from 0.1 to 1.9
- query_weight: bfloat16 [8192, 4096], P('fsdp', 'tensor'), may hold values from -2 to 2
- key_weight: bfloat16 [8192, 1024], P('fsdp', 'tensor'), may hold values from -2 to 2
- value_matrix: bfloat16 [8192, 1024], P('fsdp', 'tensor'), may hold values from -0.0625 to 0.0625
- out_weight: bfloat16 [4096, 8192], P('tensor', 'fsdp'), may hold values from -0.28125 to 0.28125
- final_gain: float32 [8192], P('tensor'), may hold values from 0.1 to 1.9
- head_weight: float32 [8192], P('tensor'), may hold values from -0.0625 to 0.0625
Outputs:
- scores: float32 [4096], P(('fsdp', 'tensor'))
- resid_out: bfloat16 [4096, 8192], P('fsdp', 'tensor')
Inputs may be any that keep to these rules, and one draw needn't show every extreme that they name: `segment_ids`: in each row, segment numbers never fall and each rollout spans 1 to 128 positions.
All inputs are finite; a program needn't handle non-finite values.
Results may differ from a plain program's by a relative error of at most 0.0071.
Values may be sent and summed in bfloat16 or wider, within the bound.
No kernel may reach another device: no remote copies, remote signals or barrier semaphores. Data moves between devices by JAX's collectives and lax.ppermute only.
A program may use at most 128 MiB of HBM per device.

v0:
```python
import functools

import jax
import jax.numpy as jnp
from jax import lax
from jax.experimental import pallas as pl
from jax.experimental.pallas import tpu as pltpu
from jax.sharding import PartitionSpec as P

MODEL_WIDTH = 8192
HEAD_SIZE = 128
EPS = 1e-05
THETA = 500000.0
NEG_FILL = -1e30
AXES = ("fsdp", "tensor")
BF = jnp.bfloat16
F32 = jnp.float32


def pairs(move):
    out = []
    for f in range(16):
        for t in range(8):
            y_hi, z, core = f // 8, (f // 2) % 4, f % 2
            y_lo, x = t // 4, t % 4
            y_hi, z, core, y_lo, x = move(y_hi, z, core, y_lo, x)
            out.append((f * 8 + t, (((y_hi % 2) * 4 + z % 4) * 2 + core % 2) * 8 + (y_lo % 2) * 4 + x % 4))
    return out


def shift(value, dy=0, dz=0, dc=0, dl=0, dx=0):
    perm = pairs(lambda h, z, c, l, x: (h + dy, z + dz, c + dc, l + dl, x + dx))
    return lax.ppermute(value, AXES, perm)


def moved(value, move):
    return lax.ppermute(value, AXES, pairs(move))


VM = pl.BlockSpec(memory_space=pltpu.VMEM)
SM = pl.BlockSpec(memory_space=pltpu.SMEM)
LIMIT = 60 * 1024 * 1024


def norm_kernel(core_ref, s_ref, g_ref, mine_ref, theirs_ref):
    core = core_ref[0]
    x = s_ref[...].astype(F32)
    scale = lax.rsqrt(jnp.sum(x * x, axis=1, keepdims=True) / MODEL_WIDTH + EPS)
    for ref, flip in ((mine_ref, core), (theirs_ref, 1 - core)):
        for j in range(8):
            cols = pl.ds(pl.multiple_of((2 * j + flip) * 512, 512), 512)
            ref[j] = (s_ref[:, cols].astype(F32) * scale * g_ref[:, cols]).astype(BF)


def normed_halves(core, states, gain):
    rows, width = states.shape
    step = 32
    out = jax.ShapeDtypeStruct((8, rows, 512), BF)
    return pl.pallas_call(
        norm_kernel,
        grid_spec=pltpu.PrefetchScalarGridSpec(
            num_scalar_prefetch=1,
            grid=(rows // step,),
            in_specs=[
                pl.BlockSpec((step, width), lambda i, c: (i, 0)),
                pl.BlockSpec((1, width), lambda i, c: (0, 0)),
            ],
            out_specs=[pl.BlockSpec((8, step, 512), lambda i, c: (0, i, 0))] * 2,
        ),
        out_shape=(out, out),
        cost_estimate=pl.CostEstimate(flops=8 * 10**9, bytes_accessed=9 * 2**20, transcendentals=0),
        name="norm",
    )(core.reshape(1), states, gain.reshape(1, width))


def project_kernel(plan, first, where_ref, *refs):
    n = sum(len(p) for p in plan)
    x_ref, got_ref = refs[0], refs[1]
    w_refs = refs[2 : 2 + n]
    rest = refs[2 + n :]
    acc_refs = rest[:2] if not first else (None, None)
    own_ref, other_ref = rest[-2:]
    rows = own_ref.shape[0]
    for side, (lo, width) in enumerate(((0, 512), (512, 256))):
        for tile in range(0, width, 256):
            acc = None
            at = 0
            for j, pieces in enumerate(plan):
                both = jnp.concatenate([x_ref[where_ref[j]], got_ref[where_ref[j]]], axis=0)
                row = 0
                for kind, depth in pieces:
                    w = w_refs[at]
                    at += 1
                    if kind != side:
                        continue
                    part = jnp.dot(both[:, row : row + depth], w[:, tile : tile + 256], preferred_element_type=F32)
                    row += depth
                    acc = part if acc is None else acc + part
            cols = slice(lo + tile, lo + tile + 256)
            if first:
                own_ref[:, cols] = acc[:rows]
                other_ref[:, cols] = acc[rows:]
            else:
                own_ref[:, cols] = acc_refs[0][:, cols] + acc[:rows]
                other_ref[:, cols] = acc_refs[1][:, cols] + acc[rows:]


def project(where, mine, got, shards, acc=None):
    plan = tuple(tuple((kind, w.shape[0]) for kind, w in pieces) for pieces in shards)
    ws = [w for pieces in shards for _, w in pieces]
    rows = mine.shape[1]
    out = jax.ShapeDtypeStruct((rows, 768), F32)
    extra = [] if acc is None else list(acc)
    return pl.pallas_call(
        functools.partial(project_kernel, plan, acc is None),
        in_specs=[SM] + [VM] * (2 + len(ws) + len(extra)),
        out_specs=(VM, VM),
        out_shape=(out, out),
        compiler_params=pltpu.CompilerParams(vmem_limit_bytes=LIMIT // 2),
        cost_estimate=pl.CostEstimate(flops=2 * 512 * 2048 * 768, bytes_accessed=2**20, transcendentals=0),
    )(where, mine, got, *ws, *extra)


def attend_kernel(a_ref, b_ref, cos_ref, sin_ref, row_ref, col_ref, out_ref):
    rows = a_ref.shape[0]
    cosine, sine = cos_ref[...], sin_ref[...]

    def rotated(at):
        x = a_ref[:, at : at + HEAD_SIZE] + b_ref[:, at : at + HEAD_SIZE]
        return (x * cosine + pltpu.roll(x, HEAD_SIZE // 2, 1) * sine).astype(BF)

    keys = rotated(512)
    values = (a_ref[:, 640:] + b_ref[:, 640:]).astype(BF)
    t = lax.broadcasted_iota(jnp.int32, (rows, rows), 0)
    s = lax.broadcasted_iota(jnp.int32, (rows, rows), 1)
    allowed = (col_ref[...] == row_ref[...]) & (s <= t)
    for h in range(4):
        q = rotated(h * HEAD_SIZE)
        logits = lax.dot_general(q, keys, (((1,), (1,)), ((), ())), preferred_element_type=F32) * HEAD_SIZE ** (-0.5)
        logits = jnp.where(allowed, logits, NEG_FILL)
        raised = jnp.exp(logits - jnp.max(logits, axis=1, keepdims=True))
        weights = (raised / jnp.sum(raised, axis=1, keepdims=True)).astype(BF)
        out_ref[:, h * HEAD_SIZE : (h + 1) * HEAD_SIZE] = jnp.dot(weights, values, preferred_element_type=F32).astype(BF)


def attended(own, other, cosine, sine, seg_row):
    rows = own.shape[0]
    return pl.pallas_call(
        attend_kernel,
        in_specs=[VM] * 6,
        out_specs=VM,
        out_shape=jax.ShapeDtypeStruct((rows, 512), BF),
        compiler_params=pltpu.CompilerParams(vmem_limit_bytes=LIMIT // 2),
        cost_estimate=pl.CostEstimate(flops=4 * 10**9, bytes_accessed=2**20, transcendentals=0),
        name="attend",
    )(own, other, cosine, sine, seg_row.reshape(1, rows), seg_row.reshape(rows, 1))


def out_kernel(where_ref, *refs):
    mixed, own, other = refs[:8], refs[8:16], refs[16:24]
    states_ref, gain_ref, head_ref, resid_ref, sums_ref, table = refs[24:]
    core = where_ref[16]
    rows = states_ref.shape[0]
    for j in range(8):
        table[where_ref[j]] = mixed[j][...]
    squares = products = None
    for side, shards in ((0, own), (1, other)):
        for tile in range(0, 512, 256):
            acc = None
            for j in range(8):
                part = jnp.dot(table[where_ref[8 + j]], shards[j][:, tile : tile + 256], preferred_element_type=F32)
                acc = part if acc is None else acc + part
            first = core if side == 0 else 1 - core
            cols = pl.ds(pl.multiple_of(first * 512 + tile, 256), 256)
            resid = (states_ref[:, cols].astype(F32) + acc).astype(BF)
            resid_ref[:, cols] = resid
            stream = resid.astype(F32)
            sq = jnp.sum(stream * stream, axis=1, keepdims=True)
            pr = jnp.sum(stream * (gain_ref[:, cols] * head_ref[:, cols]), axis=1, keepdims=True)
            squares = sq if squares is None else squares + sq
            products = pr if products is None else products + pr
    lane = lax.broadcasted_iota(jnp.int32, (rows, 128), 1)
    spread = jnp.where(lane == 0, squares, jnp.where(lane == 1, products, 0.0))
    sums_ref[...] = jnp.transpose(spread)[:8]


def finished(where, mixed, own, other, states, final_gain, head_weight):
    rows = states.shape[0]
    return pl.pallas_call(
        out_kernel,
        in_specs=[SM] + [VM] * 27,
        out_specs=(VM, VM),
        out_shape=(jax.ShapeDtypeStruct((rows, 1024), BF), jax.ShapeDtypeStruct((8, rows), F32)),
        scratch_shapes=[pltpu.VMEM((8, rows, 512), BF)],
        compiler_params=pltpu.CompilerParams(vmem_limit_bytes=LIMIT // 2),
        cost_estimate=pl.CostEstimate(flops=2 * 256 * 4096 * 1024, bytes_accessed=2**20, transcendentals=0),
        name="finish",
    )(where, *mixed, *own, *other, states, final_gain.reshape(1, 1024), head_weight.reshape(1, 1024))


def rope_tables(seg_row):
    count = seg_row.shape[0]
    places = jnp.arange(count, dtype=jnp.int32)
    boundary = jnp.concatenate([jnp.ones((1,), dtype=bool), seg_row[1:] != seg_row[:-1]])
    begins = lax.cummax(jnp.where(boundary, places, jnp.zeros_like(places)), axis=0)
    positions = (places - begins).astype(F32)
    half_width = HEAD_SIZE // 2
    frequency = THETA ** (-(2.0 * jnp.arange(half_width, dtype=F32)) / HEAD_SIZE)
    angles = positions[:, None] * frequency[None, :]
    cosine, sine = jnp.cos(angles), jnp.sin(angles)
    return (jnp.concatenate([cosine, cosine], axis=1), jnp.concatenate([-sine, sine], axis=1))


def body(
    states,
    segment_ids,
    attn_gain,
    query_weight,
    key_weight,
    value_matrix,
    out_weight,
    final_gain,
    head_weight,
):
    t_rows, _ = states.shape
    fsdp = lax.axis_index("fsdp")
    tensor = lax.axis_index("tensor")
    y_hi, z, core = fsdp // 8, (fsdp // 2) % 4, fsdp % 2
    y_lo, x = tensor // 4, tensor % 4
    half = query_weight.shape[0] // 2
    seg_row = segment_ids[0]

    def chip(dy, k):
        return ((y_hi + dy) % 2) * 4 + (z - k) % 4

    w = query_weight
    qa1, qa3, qb0 = shift(w, dz=1), shift(w, dz=-1), shift(w, dy=1)
    kv = jnp.concatenate([key_weight, value_matrix], axis=1)
    ka1, ka3, kb0 = shift(kv, dz=1), shift(kv, dz=-1), shift(kv, dy=1)
    ka2 = shift(kv, dz=2)
    turned = moved(out_weight, lambda h, z, c, l, x: (l, z + x, c, h, x))
    out_block = moved(turned, lambda h, z, c, l, x: (h, z, c, l, z - x))

    mine, theirs = normed_halves(core, states, attn_gain)
    got = shift(theirs, dc=1)

    qa2t, qa2b = shift(qa1[:half], dz=1), shift(qa3[half:], dz=-1)
    qb1, qb3 = shift(qb0, dz=1), shift(qb0, dz=-1)
    kb1, kb3 = shift(ka1, dy=1), shift(ka3, dy=1)
    kb2 = shift(ka2, dy=1)
    qb2t, qb2b = shift(qa2t, dy=1), shift(qa2b, dy=1)

    near = ((0, 0), (0, 1), (0, 3), (1, 0))
    far = ((0, 2), (1, 1), (1, 3), (1, 2))
    where = jnp.stack([chip(*p) for p in near])
    acc = project(where, mine, got, [
        [(0, w), (1, kv)], [(0, qa1), (1, ka1)], [(0, qa3), (1, ka3)], [(0, qb0), (1, kb0)]
    ])
    where = jnp.stack([chip(*p) for p in far])
    own, other = project(where, mine, got, [
        [(0, qa2t), (0, qa2b), (1, ka2)], [(0, qb1), (1, kb1)], [(0, qb3), (1, kb3)],
        [(0, qb2t), (0, qb2b), (1, kb2)],
    ], acc)
    back = shift(other, dc=1)
    cosine, sine = rope_tables(seg_row)
    mixed = attended(own, back, cosine, sine, seg_row)

    o1, o3, o2 = shift(out_block, dz=1), shift(out_block, dz=-1), shift(out_block, dz=2)
    p0 = shift(out_block, dy=1)
    p1, p3, p2 = shift(p0, dz=1), shift(p0, dz=-1), shift(o2, dy=1)
    own_out = (out_block, o1, o3, o2, p0, p1, p3, p2)
    out_places = ((0, 0), (0, 1), (0, 3), (0, 2), (1, 0), (1, 1), (1, 3), (1, 2))
    other_out = [shift(a, dc=1) for a in own_out]

    ml = shift(mixed, dl=1)
    mx = [shift(mixed, dx=k) for k in (1, 3, 2)]
    mlx = [shift(ml, dx=k) for k in (1, 3, 2)]
    pieces = [mixed, ml, *mx, *mlx]
    peers = ((0, 0), (1, 0), (0, 1), (0, 3), (0, 2), (1, 1), (1, 3), (1, 2))
    from_peer = [((y_lo + dl) % 2) * 4 + (x - k) % 4 for dl, k in peers]
    where = jnp.stack(from_peer + [((y_hi + dy) % 2) * 4 + (z - k - x) % 4 for dy, k in out_places] + [core])
    cols = lax.dynamic_slice_in_dim(states, tensor * 1024, 1024, 1)
    resid_out, sums = finished(where, pieces, own_out, other_out, cols, final_gain, head_weight)
    share = t_rows // 8
    sums = jnp.transpose(sums[:2].reshape(2, 8, share), (1, 0, 2))
    totals = lax.all_to_all(sums, "tensor", 0, 0, tiled=True).sum(axis=0)
    scores = totals[1] * lax.rsqrt(totals[0] / MODEL_WIDTH + EPS)
    return (scores, resid_out)


def solution(mesh):
    placed = (
        P("fsdp", None),
        P("fsdp", None),
        P(),
        P("fsdp", "tensor"),
        P("fsdp", "tensor"),
        P("fsdp", "tensor"),
        P("tensor", "fsdp"),
        P("tensor"),
        P("tensor"),
    )

    return jax.shard_map(
        body,
        mesh=mesh,
        in_specs=placed,
        out_specs=(P(("fsdp", "tensor")), P("fsdp", "tensor")),
        check_vma=False,
    )
```

profile of v0, /device:TPU:0, one launch (start us, length us, event | category | flops | bytes accessed | tf_op | source)
XLA Modules:
  0.0 183.8 jit_solution(18364944741791369024)
XLA Ops:
  0.6 0.9 constant_dynamic-update-slice_fusion.1
  1.6 0.9 constant_dynamic-update-slice_fusion.refs_3_
  2.5 4.2 %collective-permute-start.11 = (bf16[512,256]{1,0:T(8,128)(2,1)S(1)}, bf16[512,256]{1,0:T(8,128)(2,1)}, u32[]{:S(2)}, u32[]{:S(2)}) collective-permute-start(bf16[512,256]{1,0:T(8,128)(2,1)S(1)} %constant_dynamic-update-slice_fusion.refs_3_), channel_id=1, source_target_pairs={{0,48},{1,49},{2,50},{3,51},{4,52},{5,53},{6,54},{7,55},{8,56},{9,... | collective-permute-start | bytes 786440 | tf_op jit(solution)/shard_map/ppermute | solution.py:33
  6.7 7.5 %norm.1 = (bf16[8,256,512]{2,1,0:T(8,128)(2,1)}, bf16[8,256,512]{2,1,0:T(8,128)(2,1)}) custom-call(s32[1]{0:T(128)} %bitcast.16.core_ref, bf16[256,8192]{1,0:T(8,128)(2,1)} %s_ref.1, f32[1,8192]{1,0:T(1,128)} %bitcast.46), custom_call_target="tpu_custom_call" | custom-call | flops 8000000000 | bytes 9437184 | tf_op jit(solution)/shard_map/norm/pallas_call | solution.py:59
  14.2 3.3 %collective-permute-start.16 = (bf16[512,256]{1,0:T(8,128)(2,1)S(1)}, bf16[512,256]{1,0:T(8,128)(2,1)S(1)}, u32[]{:S(2)}, u32[]{:S(2)}) collective-permute-start(bf16[512,256]{1,0:T(8,128)(2,1)S(1)} %constant_dynamic-update-slice_fusion.refs_3_), channel_id=1, source_target_pairs={{0,64},{1,65},{2,66},{3,67},{4,68},{5,69},{6,70},{7,71},{8,72},{9,... | collective-permute-start | bytes 786440 | tf_op jit(solution)/shard_map/ppermute | solution.py:33
  17.8 1.8 collective-permute-start.5
  19.6 10.1 %collective-permute-done.8.refs_5_ = bf16[512,256]{1,0:T(8,128)(2,1)S(1)} collective-permute-done((bf16[512,256]{1,0:T(8,128)(2,1)S(1)}, bf16[512,256]{1,0:T(8,128)(2,1)S(1)}, u32[]{:S(2)}, u32[]{:S(2)}) %collective-permute-start.8) | collective-permute-done | bytes 262176 | tf_op jit(solution)/shard_map/ppermute | solution.py:33
  30.5 3.2 %collective-permute-start.3 = (bf16[512,512]{1,0:T(8,128)(2,1)}, bf16[512,512]{1,0:T(8,128)(2,1)S(1)}, u32[]{:S(2)}, u32[]{:S(2)}) collective-permute-start(bf16[512,512]{1,0:T(8,128)(2,1)} %refs_2_.1), channel_id=1, source_target_pairs={{0,48},{1,49},{2,50},{3,51},{4,52},{5,53},{6,54},{7,55},{8,56},{9,... | collective-permute-start | bytes 1572872 | tf_op jit(solution)/shard_map/ppermute | solution.py:33
  33.7 1.7 collective-permute-start.25
  35.8 3.6 %collective-permute-start.12 = (bf16[512,256]{1,0:T(8,128)(2,1)}, bf16[512,256]{1,0:T(8,128)(2,1)S(1)}, u32[]{:S(2)}, u32[]{:S(2)}) collective-permute-start(bf16[512,256]{1,0:T(8,128)(2,1)} %collective-permute-done.11.refs_7_), channel_id=1, source_target_pairs={{0,64},{1,65},{2,66},{3,67},{4,68},{5,69},{6,70},{7,71},{8,72},{9,... | collective-permute-start | bytes 786440 | tf_op jit(solution)/shard_map/ppermute | solution.py:33
  39.3 5.4 %collective-permute-done.1.refs_4_ = bf16[512,512]{1,0:T(8,128)(2,1)S(1)} collective-permute-done((bf16[512,512]{1,0:T(8,128)(2,1)}, bf16[512,512]{1,0:T(8,128)(2,1)S(1)}, u32[]{:S(2)}, u32[]{:S(2)}) %collective-permute-start.1) | collective-permute-done | bytes 524320 | tf_op jit(solution)/shard_map/ppermute | solution.py:33
  44.8 3.1 %collective-permute-start.15 = (bf16[512,256]{1,0:T(8,128)(2,1)S(1)}, bf16[512,256]{1,0:T(8,128)(2,1)S(1)}, u32[]{:S(2)}, u32[]{:S(2)}) collective-permute-start(bf16[512,256]{1,0:T(8,128)(2,1)S(1)} %collective-permute-done.5.refs_4_), channel_id=1, source_target_pairs={{0,64},{1,65},{2,66},{3,67},{4,68},{5,69},{6,70},{7,71},{8,72},{9,... | collective-permute-start | bytes 786440 | tf_op jit(solution)/shard_map/ppermute | solution.py:33
  48.6 1.5 collective-permute-start.26
  50.0 5.4 %collective-permute-done.15.refs_11_ = bf16[512,256]{1,0:T(8,128)(2,1)S(1)} collective-permute-done((bf16[512,256]{1,0:T(8,128)(2,1)S(1)}, bf16[512,256]{1,0:T(8,128)(2,1)S(1)}, u32[]{:S(2)}, u32[]{:S(2)}) %collective-permute-start.15) | collective-permute-done | bytes 262176 | tf_op jit(solution)/shard_map/ppermute | solution.py:33
  56.1 8.9 %collective-permute-start.4 = (bf16[256,512]{1,0:T(8,128)(2,1)S(1)}, bf16[256,512]{1,0:T(8,128)(2,1)S(1)}, u32[]{:S(2)}, u32[]{:S(2)}) collective-permute-start(bf16[256,512]{1,0:T(8,128)(2,1)S(1)} %slice.40), channel_id=1, source_target_pairs={{0,48},{1,49},{2,50},{3,51},{4,52},{5,53},{6,54},{7,55},{8,56},{9,... | collective-permute-start | bytes 786440 | tf_op jit(solution)/shard_map/ppermute | solution.py:33
  65.1 11.6 %collective-permute-start.13 = (bf16[256,512]{1,0:T(8,128)(2,1)S(1)}, bf16[256,512]{1,0:T(8,128)(2,1)S(1)}, u32[]{:S(2)}, u32[]{:S(2)}) collective-permute-start(bf16[256,512]{1,0:T(8,128)(2,1)S(1)} %collective-permute-done.2.refs_2_), channel_id=1, source_target_pairs={{0,64},{1,65},{2,66},{3,67},{4,68},{5,69},{6,70},{7,71},{8,72},{9,... | collective-permute-start | bytes 786440 | tf_op jit(solution)/shard_map/ppermute | solution.py:33
  78.1 2.0 %collective-permute-start.7 = (bf16[512,512]{1,0:T(8,128)(2,1)}, bf16[512,512]{1,0:T(8,128)(2,1)}, u32[]{:S(2)}, u32[]{:S(2)}) collective-permute-start(bf16[512,512]{1,0:T(8,128)(2,1)} %collective-permute-done.6.refs_8_), channel_id=1, source_target_pairs={{0,16},{1,17},{2,18},{3,19},{4,20},{5,21},{6,22},{7,23},{8,24},{9,... | collective-permute-start | bytes 1572872 | tf_op jit(solution)/shard_map/ppermute | solution.py:33
  80.1 1.0 collective-permute-done.13.refs_9_
  81.8 3.4 %collective-permute-start.14 = (bf16[256,512]{1,0:T(8,128)(2,1)S(1)}, bf16[256,512]{1,0:T(8,128)(2,1)S(1)}, u32[]{:S(2)}, u32[]{:S(2)}) collective-permute-start(bf16[256,512]{1,0:T(8,128)(2,1)S(1)} %collective-permute-done.4.refs_3_), channel_id=1, source_target_pairs={{0,64},{1,65},{2,66},{3,67},{4,68},{5,69},{6,70},{7,71},{8,72},{9,... | collective-permute-start | bytes 786440 | tf_op jit(solution)/shard_map/ppermute | solution.py:33
  86.1 6.4 %collective-permute-done.14.refs_10_ = bf16[256,512]{1,0:T(8,128)(2,1)S(1)} collective-permute-done((bf16[256,512]{1,0:T(8,128)(2,1)S(1)}, bf16[256,512]{1,0:T(8,128)(2,1)S(1)}, u32[]{:S(2)}, u32[]{:S(2)}) %collective-permute-start.14) | collective-permute-done | bytes 262176 | tf_op jit(solution)/shard_map/ppermute | solution.py:33
  93.2 3.9 %collective-permute-start.29 = (bf16[512,512]{1,0:T(8,128)(2,1)}, bf16[512,512]{1,0:T(8,128)(2,1)}, u32[]{:S(2)}, u32[]{:S(2)}) collective-permute-start(bf16[512,512]{1,0:T(8,128)(2,1)} %collective-permute-done.26.refs_8_), channel_id=1, source_target_pairs={{0,32},{1,33},{2,34},{3,35},{4,36},{5,37},{6,38},{7,39},{8,40},{9,... | collective-permute-start | bytes 1572872 | tf_op jit(solution)/shard_map/ppermute | solution.py:33
  98.6 3.3 %collective-permute-start.28 = (bf16[512,512]{1,0:T(8,128)(2,1)}, bf16[512,512]{1,0:T(8,128)(2,1)}, u32[]{:S(2)}, u32[]{:S(2)}) collective-permute-start(bf16[512,512]{1,0:T(8,128)(2,1)} %collective-permute-done.26.refs_8_), channel_id=1, source_target_pairs={{0,48},{1,49},{2,50},{3,51},{4,52},{5,53},{6,54},{7,55},{8,56},{9,... | collective-permute-start | bytes 1572872 | tf_op jit(solution)/shard_map/ppermute | solution.py:33
  102.2 1.6 copy-done
  103.8 0.9 copy-done.30
  104.8 0.9 copy-done.32
  105.8 3.2 %shard_map.104 = (f32[256,768]{1,0:T(8,128)S(1)}, f32[256,768]{1,0:T(8,128)S(1)}) custom-call(s32[4]{0:T(128)S(1)} %pad_add_fusion.1.where_ref, bf16[8,256,512]{2,1,0:T(8,128)(2,1)S(1)} %copy-done, bf16[8,256,512]{2,1,0:T(8,128)(2,1)S(1)} %collective-permute-done.refs_1_, bf16[512,512]{1,0:T(8,128)(2,1)} %refs_2_.1, ...), custom_call_target="tpu_custom_call" | custom-call | flops 1610612736 | bytes 1048576 | tf_op jit(solution)/shard_map/pallas_call | solution.py:114
  109.0 1.2 collective-permute-done.29.refs_11_
  110.2 2.1 %collective-permute-start.32 = (bf16[512,512]{1,0:T(8,128)(2,1)}, bf16[512,512]{1,0:T(8,128)(2,1)S(1)}, u32[]{:S(2)}, u32[]{:S(2)}) collective-permute-start(bf16[512,512]{1,0:T(8,128)(2,1)} %collective-permute-done.30.refs_12_), channel_id=1, source_target_pairs={{0,48},{1,49},{2,50},{3,51},{4,52},{5,53},{6,54},{7,55},{8,56},{9,... | collective-permute-start | bytes 1572872 | tf_op jit(solution)/shard_map/ppermute | solution.py:33
  112.3 5.5 %collective-permute-done.27.refs_9_ = bf16[512,512]{1,0:T(8,128)(2,1)} collective-permute-done((bf16[512,512]{1,0:T(8,128)(2,1)}, bf16[512,512]{1,0:T(8,128)(2,1)}, u32[]{:S(2)}, u32[]{:S(2)}) %collective-permute-start.27) | collective-permute-done | bytes 524320 | tf_op jit(solution)/shard_map/ppermute | solution.py:33
  117.8 2.9 %collective-permute-start.33 = (bf16[512,512]{1,0:T(8,128)(2,1)}, bf16[512,512]{1,0:T(8,128)(2,1)S(1)}, u32[]{:S(2)}, u32[]{:S(2)}) collective-permute-start(bf16[512,512]{1,0:T(8,128)(2,1)} %collective-permute-done.29.refs_11_), channel_id=1, source_target_pairs={{0,64},{1,65},{2,66},{3,67},{4,68},{5,69},{6,70},{7,71},{8,72},{9,... | collective-permute-start | bytes 1572872 | tf_op jit(solution)/shard_map/ppermute | solution.py:33
  120.8 3.8 %shard_map.105 = (f32[256,768]{1,0:T(8,128)S(1)}, f32[256,768]{1,0:T(8,128)}) custom-call(s32[4]{0:T(128)S(1)} %pad_add_fusion.where_ref, bf16[8,256,512]{2,1,0:T(8,128)(2,1)S(1)} %copy-done, bf16[8,256,512]{2,1,0:T(8,128)(2,1)S(1)} %collective-permute-done.refs_1_, bf16[256,512]{1,0:T(8,128)(2,1)S(1)} %copy-done.20, bf16[256,512]{1,0:T(8,128)(2,1)S(1)} %copy-done.24, ...), custom_call_target="tpu_custom_call" | custom-call | flops 1610612736 | bytes 1048576 | tf_op jit(solution)/shard_map/pallas_call | solution.py:114
  127.5 1.2 collective-permute-done.33.refs_15_
  130.7 1.1 copy-done.37
  131.8 2.7 %attend.1.refs_0_ = bf16[256,512]{1,0:T(8,128)(2,1)S(1)} custom-call(f32[256,768]{1,0:T(8,128)S(1)} %copy-done.37, f32[256,768]{1,0:T(8,128)} %collective-permute-done.17.b_ref, f32[256,128]{1,0:T(8,128)S(1)} %get-tuple-element.21.cos_ref, f32[256,128]{1,0:T(8,128)S(1)} %get-tuple-element.22.sin_ref, s32[1,256]{1,0:T(1,128)S(1)} %copy-done.33, ...), custom_call_target="tpu_custom_call" | custom-call | flops 4000000000 | bytes 1048576 | tf_op jit(solution)/shard_map/attend/pallas_call | solution.py:148
  134.5 1.5 collective-permute-start.18
  136.8 3.2 %collective-permute-start.20 = (bf16[256,512]{1,0:T(8,128)(2,1)S(1)}, bf16[256,512]{1,0:T(8,128)(2,1)}, u32[]{:S(2)}, u32[]{:S(2)}) collective-permute-start(bf16[256,512]{1,0:T(8,128)(2,1)S(1)} %attend.1.refs_0_), channel_id=1, source_target_pairs={{0,3},{1,0},{2,1},{3,2},{4,7},{5,4},{6,5},{7,6},{8,11},{9,8},{10,9... | collective-permute-start | bytes 786440 | tf_op jit(solution)/shard_map/ppermute | solution.py:33
  140.8 2.1 %collective-permute-done.18.refs_1_ = bf16[256,512]{1,0:T(8,128)(2,1)} collective-permute-done((bf16[256,512]{1,0:T(8,128)(2,1)S(1)}, bf16[256,512]{1,0:T(8,128)(2,1)}, u32[]{:S(2)}, u32[]{:S(2)}) %collective-permute-start.18) | collective-permute-done | bytes 262176 | tf_op jit(solution)/shard_map/ppermute | solution.py:33
  143.8 3.2 %collective-permute-start.23 = (bf16[256,512]{1,0:T(8,128)(2,1)}, bf16[256,512]{1,0:T(8,128)(2,1)}, u32[]{:S(2)}, u32[]{:S(2)}) collective-permute-start(bf16[256,512]{1,0:T(8,128)(2,1)} %collective-permute-done.18.refs_1_), channel_id=1, source_target_pairs={{0,3},{1,0},{2,1},{3,2},{4,7},{5,4},{6,5},{7,6},{8,11},{9,8},{10,9... | collective-permute-start | bytes 786440 | tf_op jit(solution)/shard_map/ppermute | solution.py:33
  148.0 1.1 constant_dynamic-slice_fusion.refs_24_
  149.0 3.2 %collective-permute-done.20.refs_3_ = bf16[256,512]{1,0:T(8,128)(2,1)} collective-permute-done((bf16[256,512]{1,0:T(8,128)(2,1)S(1)}, bf16[256,512]{1,0:T(8,128)(2,1)}, u32[]{:S(2)}, u32[]{:S(2)}) %collective-permute-start.20) | collective-permute-done | bytes 262176 | tf_op jit(solution)/shard_map/ppermute | solution.py:33
  152.3 5.2 %collective-permute-done.22.refs_5_ = bf16[256,512]{1,0:T(8,128)(2,1)} collective-permute-done((bf16[256,512]{1,0:T(8,128)(2,1)}, bf16[256,512]{1,0:T(8,128)(2,1)}, u32[]{:S(2)}, u32[]{:S(2)}) %collective-permute-start.22) | collective-permute-done | bytes 262176 | tf_op jit(solution)/shard_map/ppermute | solution.py:33
  157.5 4.8 %collective-permute-done.23.refs_6_ = bf16[256,512]{1,0:T(8,128)(2,1)} collective-permute-done((bf16[256,512]{1,0:T(8,128)(2,1)}, bf16[256,512]{1,0:T(8,128)(2,1)}, u32[]{:S(2)}, u32[]{:S(2)}) %collective-permute-start.23) | collective-permute-done | bytes 262176 | tf_op jit(solution)/shard_map/ppermute | solution.py:33
  162.2 1.0 copy-done.4
  163.3 1.0 copy-done.6
  164.3 1.0 copy-done.8
  165.4 0.9 copy-done.12
  166.3 5.8 %finish.1 = (bf16[256,1024]{1,0:T(8,128)(2,1)}, f32[8,256]{1,0:T(8,128)S(1)}) custom-call(s32[17]{0:T(128)S(1)} %stack.101.where_ref, bf16[256,512]{1,0:T(8,128)(2,1)S(1)} %attend.1.refs_0_, bf16[256,512]{1,0:T(8,128)(2,1)} %collective-permute-done.18.refs_1_, bf16[256,512]{1,0:T(8,128)(2,1)S(1)} %copy-done.12, ...), custom_call_target="tpu_custom_call" | custom-call | flops 2147483648 | bytes 1048576 | tf_op jit(solution)/shard_map/finish/pallas_call | solution.py:189
  172.2 11.0 %all_to_all.5 = f32[8,2,32]{2,1,0:T(2,128)S(1)} all-to-all(f32[8,2,32]{2,1,0:T(2,128)S(1)} %bitcast.45), channel_id=1, replica_groups=mesh['fsdp'=16,'tensor'=8] {'tensor'}, dimensions={0} | all-to-all | bytes 4096 | tf_op jit(solution)/shard_map/all_to_all | solution.py:286
  (142 shorter events, 17.1 us)
Async XLA Ops:
  2.5 15.3 %collective-permute-start.11 = (bf16[512,256]{1,0:T(8,128)(2,1)S(1)}, bf16[512,256]{1,0:T(8,128)(2,1)}, u32[]{:S(2)}, u32[]{:S(2)}) collective-permute-start(bf16[512,256]{1,0:T(8,128)(2,1)S(1)} %constant_dynamic-update-slice_fusion.refs_3_), channel_id=1, source_target_pairs={{0,48},{1,49},{2,50},{3,51},{4,52},{5,53},{6,54},{7,55},{8,56},{9,... | collective-permute-start | bytes 786440 | tf_op jit(solution)/shard_map/ppermute | solution.py:33
  6.7 91.2 %copy-start.33 = (s32[1,256]{1,0:T(1,128)S(1)}, s32[1,256]{1,0:T(1,128)}, u32[]{:S(2)}) copy-start(s32[1,256]{1,0:T(1,128)} %row_ref.1) | copy-start | bytes 3076
  14.2 87.9 %collective-permute-start = (bf16[8,256,512]{2,1,0:T(8,128)(2,1)}, bf16[8,256,512]{2,1,0:T(8,128)(2,1)S(1)}, u32[]{:S(2)}, u32[]{:S(2)}) collective-permute-start(bf16[8,256,512]{2,1,0:T(8,128)(2,1)} %get-tuple-element.11), channel_id=1, source_target_pairs={{0,8},{1,9},{2,10},{3,11},{4,12},{5,13},{6,14},{7,15},{8,0},{9,1},... | collective-permute-start | bytes 6291464 | tf_op jit(solution)/shard_map/ppermute | solution.py:33
  14.2 15.5 %collective-permute-start.8 = (bf16[512,256]{1,0:T(8,128)(2,1)S(1)}, bf16[512,256]{1,0:T(8,128)(2,1)S(1)}, u32[]{:S(2)}, u32[]{:S(2)}) collective-permute-start(bf16[512,256]{1,0:T(8,128)(2,1)S(1)} %constant_dynamic-update-slice_fusion.refs_3_), channel_id=1, source_target_pairs={{0,16},{1,17},{2,18},{3,19},{4,20},{5,21},{6,22},{7,23},{8,24},{9,... | collective-permute-start | bytes 786440 | tf_op jit(solution)/shard_map/ppermute | solution.py:33
  14.2 15.5 %collective-permute-start.16 = (bf16[512,256]{1,0:T(8,128)(2,1)S(1)}, bf16[512,256]{1,0:T(8,128)(2,1)S(1)}, u32[]{:S(2)}, u32[]{:S(2)}) collective-permute-start(bf16[512,256]{1,0:T(8,128)(2,1)S(1)} %constant_dynamic-update-slice_fusion.refs_3_), channel_id=1, source_target_pairs={{0,64},{1,65},{2,66},{3,67},{4,68},{5,69},{6,70},{7,71},{8,72},{9,... | collective-permute-start | bytes 786440 | tf_op jit(solution)/shard_map/ppermute | solution.py:33
  17.5 18.3 %collective-permute-start.6 = (bf16[512,512]{1,0:T(8,128)(2,1)}, bf16[512,512]{1,0:T(8,128)(2,1)}, u32[]{:S(2)}, u32[]{:S(2)}) collective-permute-start(bf16[512,512]{1,0:T(8,128)(2,1)} %refs_2_.1), channel_id=1, source_target_pairs={{0,64},{1,65},{2,66},{3,67},{4,68},{5,69},{6,70},{7,71},{8,72},{9,... | collective-permute-start | bytes 1572872 | tf_op jit(solution)/shard_map/ppermute | solution.py:33
  17.8 15.9 %collective-permute-start.5 = (bf16[512,256]{1,0:T(8,128)(2,1)S(1)}, bf16[512,256]{1,0:T(8,128)(2,1)S(1)}, u32[]{:S(2)}, u32[]{:S(2)}) collective-permute-start(bf16[512,256]{1,0:T(8,128)(2,1)S(1)} %constant_dynamic-update-slice_fusion.refs_3_), channel_id=1, source_target_pairs={{0,32},{1,33},{2,34},{3,35},{4,36},{5,37},{6,38},{7,39},{8,40},{9,... | collective-permute-start | bytes 786440 | tf_op jit(solution)/shard_map/ppermute | solution.py:33
  29.8 68.1 %copy-start.29 = (bf16[512,256]{1,0:T(8,128)(2,1)}, bf16[512,256]{1,0:T(8,128)(2,1)S(1)}, u32[]{:S(2)}) copy-start(bf16[512,256]{1,0:T(8,128)(2,1)S(1)} %collective-permute-done.8.refs_5_) | copy-start | bytes 786436
  29.8 15.0 %collective-permute-start.1 = (bf16[512,512]{1,0:T(8,128)(2,1)}, bf16[512,512]{1,0:T(8,128)(2,1)S(1)}, u32[]{:S(2)}, u32[]{:S(2)}) collective-permute-start(bf16[512,512]{1,0:T(8,128)(2,1)} %refs_2_.1), channel_id=1, source_target_pairs={{0,16},{1,17},{2,18},{3,19},{4,20},{5,21},{6,22},{7,23},{8,24},{9,... | collective-permute-start | bytes 1572872 | tf_op jit(solution)/shard_map/ppermute | solution.py:33
  30.5 17.4 %collective-permute-start.3 = (bf16[512,512]{1,0:T(8,128)(2,1)}, bf16[512,512]{1,0:T(8,128)(2,1)S(1)}, u32[]{:S(2)}, u32[]{:S(2)}) collective-permute-start(bf16[512,512]{1,0:T(8,128)(2,1)} %refs_2_.1), channel_id=1, source_target_pairs={{0,48},{1,49},{2,50},{3,51},{4,52},{5,53},{6,54},{7,55},{8,56},{9,... | collective-permute-start | bytes 1572872 | tf_op jit(solution)/shard_map/ppermute | solution.py:33
  33.7 63.4 %copy-start.13 = (bf16[512,256]{1,0:T(8,128)(2,1)}, bf16[512,256]{1,0:T(8,128)(2,1)S(1)}, u32[]{:S(2)}) copy-start(bf16[512,256]{1,0:T(8,128)(2,1)S(1)} %collective-permute-done.5.refs_4_) | copy-start | bytes 786436
  33.7 14.9 %collective-permute-start.25 = (bf16[512,512]{1,0:T(8,128)(2,1)}, bf16[512,512]{1,0:T(8,128)(2,1)S(1)}, u32[]{:S(2)}, u32[]{:S(2)}) collective-permute-start(bf16[512,512]{1,0:T(8,128)(2,1)} %param.15), channel_id=1, source_target_pairs={{0,0},{1,17},{2,34},{3,51},{4,64},{5,81},{6,98},{7,115},{8,8},{9,2... | collective-permute-start | bytes 1572872 | tf_op jit(solution)/shard_map/ppermute | solution.py:37
  35.8 12.2 %collective-permute-start.12 = (bf16[512,256]{1,0:T(8,128)(2,1)}, bf16[512,256]{1,0:T(8,128)(2,1)S(1)}, u32[]{:S(2)}, u32[]{:S(2)}) collective-permute-start(bf16[512,256]{1,0:T(8,128)(2,1)} %collective-permute-done.11.refs_7_), channel_id=1, source_target_pairs={{0,64},{1,65},{2,66},{3,67},{4,68},{5,69},{6,70},{7,71},{8,72},{9,... | collective-permute-start | bytes 786440 | tf_op jit(solution)/shard_map/ppermute | solution.py:33
  44.8 10.7 %collective-permute-start.15 = (bf16[512,256]{1,0:T(8,128)(2,1)S(1)}, bf16[512,256]{1,0:T(8,128)(2,1)S(1)}, u32[]{:S(2)}, u32[]{:S(2)}) collective-permute-start(bf16[512,256]{1,0:T(8,128)(2,1)S(1)} %collective-permute-done.5.refs_4_), channel_id=1, source_target_pairs={{0,64},{1,65},{2,66},{3,67},{4,68},{5,69},{6,70},{7,71},{8,72},{9,... | collective-permute-start | bytes 786440 | tf_op jit(solution)/shard_map/ppermute | solution.py:33
  47.9 17.2 %collective-permute-start.2 = (bf16[256,512]{1,0:T(8,128)(2,1)S(1)}, bf16[256,512]{1,0:T(8,128)(2,1)S(1)}, u32[]{:S(2)}, u32[]{:S(2)}) collective-permute-start(bf16[256,512]{1,0:T(8,128)(2,1)S(1)} %slice.39), channel_id=1, source_target_pairs={{0,16},{1,17},{2,18},{3,19},{4,20},{5,21},{6,22},{7,23},{8,24},{9,... | collective-permute-start | bytes 786440 | tf_op jit(solution)/shard_map/ppermute | solution.py:33
  48.0 49.9 %copy-start.15 = (bf16[512,256]{1,0:T(8,128)(2,1)}, bf16[512,256]{1,0:T(8,128)(2,1)S(1)}, u32[]{:S(2)}) copy-start(bf16[512,256]{1,0:T(8,128)(2,1)S(1)} %collective-permute-done.12.refs_8_) | copy-start | bytes 786436
  48.0 29.4 %collective-permute-start.9 = (bf16[512,256]{1,0:T(8,128)(2,1)S(1)}, bf16[512,256]{1,0:T(8,128)(2,1)S(1)}, u32[]{:S(2)}, u32[]{:S(2)}) collective-permute-start(bf16[512,256]{1,0:T(8,128)(2,1)S(1)} %collective-permute-done.8.refs_5_), channel_id=1, source_target_pairs={{0,64},{1,65},{2,66},{3,67},{4,68},{5,69},{6,70},{7,71},{8,72},{9,... | collective-permute-start | bytes 786440 | tf_op jit(solution)/shard_map/ppermute | solution.py:33
  48.6 37.4 %collective-permute-start.26 = (bf16[512,512]{1,0:T(8,128)(2,1)S(1)}, bf16[512,512]{1,0:T(8,128)(2,1)}, u32[]{:S(2)}, u32[]{:S(2)}) collective-permute-start(bf16[512,512]{1,0:T(8,128)(2,1)S(1)} %collective-permute-done.25), channel_id=1, source_target_pairs={{0,0},{1,3},{2,2},{3,1},{4,4},{5,7},{6,6},{7,5},{8,8},{9,11},{10,1... | collective-permute-start | bytes 1572872 | tf_op jit(solution)/shard_map/ppermute | solution.py:37
  56.1 21.9 %collective-permute-start.4 = (bf16[256,512]{1,0:T(8,128)(2,1)S(1)}, bf16[256,512]{1,0:T(8,128)(2,1)S(1)}, u32[]{:S(2)}, u32[]{:S(2)}) collective-permute-start(bf16[256,512]{1,0:T(8,128)(2,1)S(1)} %slice.40), channel_id=1, source_target_pairs={{0,48},{1,49},{2,50},{3,51},{4,52},{5,53},{6,54},{7,55},{8,56},{9,... | collective-permute-start | bytes 786440 | tf_op jit(solution)/shard_map/ppermute | solution.py:33
  65.1 16.1 %collective-permute-start.13 = (bf16[256,512]{1,0:T(8,128)(2,1)S(1)}, bf16[256,512]{1,0:T(8,128)(2,1)S(1)}, u32[]{:S(2)}, u32[]{:S(2)}) collective-permute-start(bf16[256,512]{1,0:T(8,128)(2,1)S(1)} %collective-permute-done.2.refs_2_), channel_id=1, source_target_pairs={{0,64},{1,65},{2,66},{3,67},{4,68},{5,69},{6,70},{7,71},{8,72},{9,... | collective-permute-start | bytes 786440 | tf_op jit(solution)/shard_map/ppermute | solution.py:33
  78.1 19.0 %collective-permute-start.10 = (bf16[512,512]{1,0:T(8,128)(2,1)}, bf16[512,512]{1,0:T(8,128)(2,1)S(1)}, u32[]{:S(2)}, u32[]{:S(2)}) collective-permute-start(bf16[512,512]{1,0:T(8,128)(2,1)} %collective-permute-done.6.refs_8_), channel_id=1, source_target_pairs={{0,48},{1,49},{2,50},{3,51},{4,52},{5,53},{6,54},{7,55},{8,56},{9,... | collective-permute-start | bytes 1572872 | tf_op jit(solution)/shard_map/ppermute | solution.py:33
  78.1 20.6 %collective-permute-start.7 = (bf16[512,512]{1,0:T(8,128)(2,1)}, bf16[512,512]{1,0:T(8,128)(2,1)}, u32[]{:S(2)}, u32[]{:S(2)}) collective-permute-start(bf16[512,512]{1,0:T(8,128)(2,1)} %collective-permute-done.6.refs_8_), channel_id=1, source_target_pairs={{0,16},{1,17},{2,18},{3,19},{4,20},{5,21},{6,22},{7,23},{8,24},{9,... | collective-permute-start | bytes 1572872 | tf_op jit(solution)/shard_map/ppermute | solution.py:33
  81.8 10.7 %collective-permute-start.14 = (bf16[256,512]{1,0:T(8,128)(2,1)S(1)}, bf16[256,512]{1,0:T(8,128)(2,1)S(1)}, u32[]{:S(2)}, u32[]{:S(2)}) collective-permute-start(bf16[256,512]{1,0:T(8,128)(2,1)S(1)} %collective-permute-done.4.refs_3_), channel_id=1, source_target_pairs={{0,64},{1,65},{2,66},{3,67},{4,68},{5,69},{6,70},{7,71},{8,72},{9,... | collective-permute-start | bytes 786440 | tf_op jit(solution)/shard_map/ppermute | solution.py:33
  86.0 16.1 %collective-permute-start.30 = (bf16[512,512]{1,0:T(8,128)(2,1)}, bf16[512,512]{1,0:T(8,128)(2,1)}, u32[]{:S(2)}, u32[]{:S(2)}) collective-permute-start(bf16[512,512]{1,0:T(8,128)(2,1)} %collective-permute-done.26.refs_8_), channel_id=1, source_target_pairs={{0,64},{1,65},{2,66},{3,67},{4,68},{5,69},{6,70},{7,71},{8,72},{9,... | collective-permute-start | bytes 1572872 | tf_op jit(solution)/shard_map/ppermute | solution.py:33
  93.2 16.9 %collective-permute-start.29 = (bf16[512,512]{1,0:T(8,128)(2,1)}, bf16[512,512]{1,0:T(8,128)(2,1)}, u32[]{:S(2)}, u32[]{:S(2)}) collective-permute-start(bf16[512,512]{1,0:T(8,128)(2,1)} %collective-permute-done.26.refs_8_), channel_id=1, source_target_pairs={{0,32},{1,33},{2,34},{3,35},{4,36},{5,37},{6,38},{7,39},{8,40},{9,... | collective-permute-start | bytes 1572872 | tf_op jit(solution)/shard_map/ppermute | solution.py:33
  97.9 19.9 %collective-permute-start.27 = (bf16[512,512]{1,0:T(8,128)(2,1)}, bf16[512,512]{1,0:T(8,128)(2,1)}, u32[]{:S(2)}, u32[]{:S(2)}) collective-permute-start(bf16[512,512]{1,0:T(8,128)(2,1)} %collective-permute-done.26.refs_8_), channel_id=1, source_target_pairs={{0,16},{1,17},{2,18},{3,19},{4,20},{5,21},{6,22},{7,23},{8,24},{9,... | collective-permute-start | bytes 1572872 | tf_op jit(solution)/shard_map/ppermute | solution.py:33
  98.6 26.8 %collective-permute-start.28 = (bf16[512,512]{1,0:T(8,128)(2,1)}, bf16[512,512]{1,0:T(8,128)(2,1)}, u32[]{:S(2)}, u32[]{:S(2)}) collective-permute-start(bf16[512,512]{1,0:T(8,128)(2,1)} %collective-permute-done.26.refs_8_), channel_id=1, source_target_pairs={{0,48},{1,49},{2,50},{3,51},{4,52},{5,53},{6,54},{7,55},{8,56},{9,... | collective-permute-start | bytes 1572872 | tf_op jit(solution)/shard_map/ppermute | solution.py:33
  102.1 23.5 %collective-permute-start.34 = (bf16[512,512]{1,0:T(8,128)(2,1)}, bf16[512,512]{1,0:T(8,128)(2,1)S(1)}, u32[]{:S(2)}, u32[]{:S(2)}) collective-permute-start(bf16[512,512]{1,0:T(8,128)(2,1)} %collective-permute-done.26.refs_8_), channel_id=1, source_target_pairs={{0,8},{1,9},{2,10},{3,11},{4,12},{5,13},{6,14},{7,15},{8,0},{9,1},... | collective-permute-start | bytes 1572872 | tf_op jit(solution)/shard_map/ppermute | solution.py:33
  102.1 24.8 %collective-permute-start.31 = (bf16[512,512]{1,0:T(8,128)(2,1)}, bf16[512,512]{1,0:T(8,128)(2,1)}, u32[]{:S(2)}, u32[]{:S(2)}) collective-permute-start(bf16[512,512]{1,0:T(8,128)(2,1)} %collective-permute-done.30.refs_12_), channel_id=1, source_target_pairs={{0,16},{1,17},{2,18},{3,19},{4,20},{5,21},{6,22},{7,23},{8,24},{9,... | collective-permute-start | bytes 1572872 | tf_op jit(solution)/shard_map/ppermute | solution.py:33
  110.2 16.8 %collective-permute-start.32 = (bf16[512,512]{1,0:T(8,128)(2,1)}, bf16[512,512]{1,0:T(8,128)(2,1)S(1)}, u32[]{:S(2)}, u32[]{:S(2)}) collective-permute-start(bf16[512,512]{1,0:T(8,128)(2,1)} %collective-permute-done.30.refs_12_), channel_id=1, source_target_pairs={{0,48},{1,49},{2,50},{3,51},{4,52},{5,53},{6,54},{7,55},{8,56},{9,... | collective-permute-start | bytes 1572872 | tf_op jit(solution)/shard_map/ppermute | solution.py:33
  117.8 10.9 %collective-permute-start.33 = (bf16[512,512]{1,0:T(8,128)(2,1)}, bf16[512,512]{1,0:T(8,128)(2,1)S(1)}, u32[]{:S(2)}, u32[]{:S(2)}) collective-permute-start(bf16[512,512]{1,0:T(8,128)(2,1)} %collective-permute-done.29.refs_11_), channel_id=1, source_target_pairs={{0,64},{1,65},{2,66},{3,67},{4,68},{5,69},{6,70},{7,71},{8,72},{9,... | collective-permute-start | bytes 1572872 | tf_op jit(solution)/shard_map/ppermute | solution.py:33
  125.5 4.8 %collective-permute-start.17 = (f32[256,768]{1,0:T(8,128)}, f32[256,768]{1,0:T(8,128)}, u32[]{:S(2)}, u32[]{:S(2)}) collective-permute-start(f32[256,768]{1,0:T(8,128)} %get-tuple-element.15), channel_id=1, source_target_pairs={{0,8},{1,9},{2,10},{3,11},{4,12},{5,13},{6,14},{7,15},{8,0},{9,1},... | collective-permute-start | bytes 2359304 | tf_op jit(solution)/shard_map/ppermute | solution.py:33
  126.4 3.1 %collective-permute-start.38 = (bf16[512,512]{1,0:T(8,128)(2,1)}, bf16[512,512]{1,0:T(8,128)(2,1)S(1)}, u32[]{:S(2)}, u32[]{:S(2)}) collective-permute-start(bf16[512,512]{1,0:T(8,128)(2,1)} %collective-permute-done.30.refs_12_), channel_id=1, source_target_pairs={{0,8},{1,9},{2,10},{3,11},{4,12},{5,13},{6,14},{7,15},{8,0},{9,1},... | collective-permute-start | bytes 1572872 | tf_op jit(solution)/shard_map/ppermute | solution.py:33
  126.9 3.2 %collective-permute-start.37 = (bf16[512,512]{1,0:T(8,128)(2,1)}, bf16[512,512]{1,0:T(8,128)(2,1)S(1)}, u32[]{:S(2)}, u32[]{:S(2)}) collective-permute-start(bf16[512,512]{1,0:T(8,128)(2,1)} %collective-permute-done.29.refs_11_), channel_id=1, source_target_pairs={{0,8},{1,9},{2,10},{3,11},{4,12},{5,13},{6,14},{7,15},{8,0},{9,1},... | collective-permute-start | bytes 1572872 | tf_op jit(solution)/shard_map/ppermute | solution.py:33
  127.0 7.5 %collective-permute-start.35 = (bf16[512,512]{1,0:T(8,128)(2,1)}, bf16[512,512]{1,0:T(8,128)(2,1)S(1)}, u32[]{:S(2)}, u32[]{:S(2)}) collective-permute-start(bf16[512,512]{1,0:T(8,128)(2,1)} %collective-permute-done.27.refs_9_), channel_id=1, source_target_pairs={{0,8},{1,9},{2,10},{3,11},{4,12},{5,13},{6,14},{7,15},{8,0},{9,1},... | collective-permute-start | bytes 1572872 | tf_op jit(solution)/shard_map/ppermute | solution.py:33
  128.7 7.2 %collective-permute-start.36 = (bf16[512,512]{1,0:T(8,128)(2,1)}, bf16[512,512]{1,0:T(8,128)(2,1)}, u32[]{:S(2)}, u32[]{:S(2)}) collective-permute-start(bf16[512,512]{1,0:T(8,128)(2,1)} %collective-permute-done.28.refs_10_), channel_id=1, source_target_pairs={{0,8},{1,9},{2,10},{3,11},{4,12},{5,13},{6,14},{7,15},{8,0},{9,1},... | collective-permute-start | bytes 1572872 | tf_op jit(solution)/shard_map/ppermute | solution.py:33
  129.5 6.4 %collective-permute-start.39 = (bf16[512,512]{1,0:T(8,128)(2,1)}, bf16[512,512]{1,0:T(8,128)(2,1)S(1)}, u32[]{:S(2)}, u32[]{:S(2)}) collective-permute-start(bf16[512,512]{1,0:T(8,128)(2,1)} %collective-permute-done.31.refs_13_), channel_id=1, source_target_pairs={{0,8},{1,9},{2,10},{3,11},{4,12},{5,13},{6,14},{7,15},{8,0},{9,1},... | collective-permute-start | bytes 1572872 | tf_op jit(solution)/shard_map/ppermute | solution.py:33
  130.1 9.9 %collective-permute-start.40 = (bf16[512,512]{1,0:T(8,128)(2,1)S(1)}, bf16[512,512]{1,0:T(8,128)(2,1)S(1)}, u32[]{:S(2)}, u32[]{:S(2)}) collective-permute-start(bf16[512,512]{1,0:T(8,128)(2,1)S(1)} %collective-permute-done.32.refs_14_), channel_id=1, source_target_pairs={{0,8},{1,9},{2,10},{3,11},{4,12},{5,13},{6,14},{7,15},{8,0},{9,1},... | collective-permute-start | bytes 1572872 | tf_op jit(solution)/shard_map/ppermute | solution.py:33
  130.2 12.7 %collective-permute-start.41 = (bf16[512,512]{1,0:T(8,128)(2,1)S(1)}, bf16[512,512]{1,0:T(8,128)(2,1)S(1)}, u32[]{:S(2)}, u32[]{:S(2)}) collective-permute-start(bf16[512,512]{1,0:T(8,128)(2,1)S(1)} %collective-permute-done.33.refs_15_), channel_id=1, source_target_pairs={{0,8},{1,9},{2,10},{3,11},{4,12},{5,13},{6,14},{7,15},{8,0},{9,1},... | collective-permute-start | bytes 1572872 | tf_op jit(solution)/shard_map/ppermute | solution.py:33
  131.8 30.4 %copy-start.34 = (f32[1024]{0:T(1024)S(1)}, f32[1024]{0:T(1024)}, u32[]{:S(2)}) copy-start(f32[1024]{0:T(1024)} %param.16) | copy-start | bytes 12292
  131.8 30.4 %copy-start.35 = (f32[1024]{0:T(1024)S(1)}, f32[1024]{0:T(1024)}, u32[]{:S(2)}) copy-start(f32[1024]{0:T(1024)} %param.17) | copy-start | bytes 12292
  134.5 8.5 %collective-permute-start.18 = (bf16[256,512]{1,0:T(8,128)(2,1)S(1)}, bf16[256,512]{1,0:T(8,128)(2,1)}, u32[]{:S(2)}, u32[]{:S(2)}) collective-permute-start(bf16[256,512]{1,0:T(8,128)(2,1)S(1)} %attend.1.refs_0_), channel_id=1, source_target_pairs={{0,4},{1,5},{2,6},{3,7},{4,0},{5,1},{6,2},{7,3},{8,12},{9,13},{10,... | collective-permute-start | bytes 786440 | tf_op jit(solution)/shard_map/ppermute | solution.py:33
  135.9 11.0 %collective-permute-start.19 = (bf16[256,512]{1,0:T(8,128)(2,1)S(1)}, bf16[256,512]{1,0:T(8,128)(2,1)S(1)}, u32[]{:S(2)}, u32[]{:S(2)}) collective-permute-start(bf16[256,512]{1,0:T(8,128)(2,1)S(1)} %attend.1.refs_0_), channel_id=1, source_target_pairs={{0,1},{1,2},{2,3},{3,0},{4,5},{5,6},{6,7},{7,4},{8,9},{9,10},{10,1... | collective-permute-start | bytes 786440 | tf_op jit(solution)/shard_map/ppermute | solution.py:33
  136.8 15.5 %collective-permute-start.20 = (bf16[256,512]{1,0:T(8,128)(2,1)S(1)}, bf16[256,512]{1,0:T(8,128)(2,1)}, u32[]{:S(2)}, u32[]{:S(2)}) collective-permute-start(bf16[256,512]{1,0:T(8,128)(2,1)S(1)} %attend.1.refs_0_), channel_id=1, source_target_pairs={{0,3},{1,0},{2,1},{3,2},{4,7},{5,4},{6,5},{7,6},{8,11},{9,8},{10,9... | collective-permute-start | bytes 786440 | tf_op jit(solution)/shard_map/ppermute | solution.py:33
  140.8 11.5 %collective-permute-start.21 = (bf16[256,512]{1,0:T(8,128)(2,1)S(1)}, bf16[256,512]{1,0:T(8,128)(2,1)}, u32[]{:S(2)}, u32[]{:S(2)}) collective-permute-start(bf16[256,512]{1,0:T(8,128)(2,1)S(1)} %attend.1.refs_0_), channel_id=1, source_target_pairs={{0,2},{1,3},{2,0},{3,1},{4,6},{5,7},{6,4},{7,5},{8,10},{9,11},{10,... | collective-permute-start | bytes 786440 | tf_op jit(solution)/shard_map/ppermute | solution.py:33
  142.9 14.5 %collective-permute-start.22 = (bf16[256,512]{1,0:T(8,128)(2,1)}, bf16[256,512]{1,0:T(8,128)(2,1)}, u32[]{:S(2)}, u32[]{:S(2)}) collective-permute-start(bf16[256,512]{1,0:T(8,128)(2,1)} %collective-permute-done.18.refs_1_), channel_id=1, source_target_pairs={{0,1},{1,2},{2,3},{3,0},{4,5},{5,6},{6,7},{7,4},{8,9},{9,10},{10,1... | collective-permute-start | bytes 786440 | tf_op jit(solution)/shard_map/ppermute | solution.py:33
  143.8 18.5 %collective-permute-start.23 = (bf16[256,512]{1,0:T(8,128)(2,1)}, bf16[256,512]{1,0:T(8,128)(2,1)}, u32[]{:S(2)}, u32[]{:S(2)}) collective-permute-start(bf16[256,512]{1,0:T(8,128)(2,1)} %collective-permute-done.18.refs_1_), channel_id=1, source_target_pairs={{0,3},{1,0},{2,1},{3,2},{4,7},{5,4},{6,5},{7,6},{8,11},{9,8},{10,9... | collective-permute-start | bytes 786440 | tf_op jit(solution)/shard_map/ppermute | solution.py:33
  147.7 14.5 %collective-permute-start.24 = (bf16[256,512]{1,0:T(8,128)(2,1)}, bf16[256,512]{1,0:T(8,128)(2,1)}, u32[]{:S(2)}, u32[]{:S(2)}) collective-permute-start(bf16[256,512]{1,0:T(8,128)(2,1)} %collective-permute-done.18.refs_1_), channel_id=1, source_target_pairs={{0,2},{1,3},{2,0},{3,1},{4,6},{5,7},{6,4},{7,5},{8,10},{9,11},{10,... | collective-permute-start | bytes 786440 | tf_op jit(solution)/shard_map/ppermute | solution.py:33
  (32 other events, 184.9 us)
where the time goes:
time: 185 us; the launch traced here: 184 us
  starting transfers between devices  71.9 us (39%)
  waiting for transfers between devices  52.1 us (28%)
  Pallas kernels  23 us (12%)
  local copies, waits for them, and re-layouts  22.7 us (12%)
  blocking collectives  11 us (6%)
  other arithmetic  1.97 us (1%)
    ppermute x40, starting transfers between devices, shift(): return lax.ppermute(value, AXES, perm)  68.8 us
    ppermute x40, waiting for transfers between devices, shift(): return lax.ppermute(value, AXES, perm)  52.1 us
    unnamed x77, local copies, waits for them, and re-layouts  20.2 us
    all_to_all x1, blocking collectives, body(): totals = lax.all_to_all(sums, 'tensor', 0, 0, tiled=True).sum(axis=0)  11 us
    pallas_call x1, Pallas kernels, normed_halves(): pl.pallas_call(norm_kernel, grid_spec=pltpu.PrefetchScalarGridSpec(num_sc...  7.48 us
    pallas_call x2, Pallas kernels, project(): pl.pallas_call(functools.partial(project_kernel, plan, acc is None), in_s...  7.01 us
    pallas_call x1, Pallas kernels, finished(): pl.pallas_call(out_kernel, in_specs=[SM] + [VM] * 27, out_specs=(VM, VM),...  5.81 us
  transfers between devices with their start and end apart: 42, of which 13 were waited for; matrix products, arithmetic and copies ran while one was open for 2% of the time, Pallas kernels for 9%

commit v1 on v0

--- a/solution.py
+++ b/solution.py
@@ -39,7 +39,6 @@
 
 VM = pl.BlockSpec(memory_space=pltpu.VMEM)
 SM = pl.BlockSpec(memory_space=pltpu.SMEM)
-LIMIT = 60 * 1024 * 1024
 
 
 def norm_kernel(core_ref, s_ref, g_ref, mine_ref, theirs_ref):
@@ -68,6 +67,7 @@
             out_specs=[pl.BlockSpec((8, step, 512), lambda i, c: (0, i, 0))] * 2,
         ),
         out_shape=(out, out),
+        compiler_params=pltpu.CompilerParams(vmem_limit_bytes=16 * 2**20),
         cost_estimate=pl.CostEstimate(flops=8 * 10**9, bytes_accessed=9 * 2**20, transcendentals=0),
         name="norm",
     )(core.reshape(1), states, gain.reshape(1, width))
@@ -116,7 +116,7 @@
         in_specs=[SM] + [VM] * (2 + len(ws) + len(extra)),
         out_specs=(VM, VM),
         out_shape=(out, out),
-        compiler_params=pltpu.CompilerParams(vmem_limit_bytes=LIMIT // 2),
+        compiler_params=pltpu.CompilerParams(vmem_limit_bytes=16 * 2**20),
         cost_estimate=pl.CostEstimate(flops=2 * 512 * 2048 * 768, bytes_accessed=2**20, transcendentals=0),
     )(where, mine, got, *ws, *extra)
 
@@ -150,52 +150,81 @@
         in_specs=[VM] * 6,
         out_specs=VM,
         out_shape=jax.ShapeDtypeStruct((rows, 512), BF),
-        compiler_params=pltpu.CompilerParams(vmem_limit_bytes=LIMIT // 2),
+        compiler_params=pltpu.CompilerParams(vmem_limit_bytes=16 * 2**20),
         cost_estimate=pl.CostEstimate(flops=4 * 10**9, bytes_accessed=2**20, transcendentals=0),
         name="attend",
     )(own, other, cosine, sine, seg_row.reshape(1, rows), seg_row.reshape(rows, 1))
 
 
-def out_kernel(where_ref, *refs):
-    mixed, own, other = refs[:8], refs[8:16], refs[16:24]
-    states_ref, gain_ref, head_ref, resid_ref, sums_ref, table = refs[24:]
-    core = where_ref[16]
-    rows = states_ref.shape[0]
-    for j in range(8):
-        table[where_ref[j]] = mixed[j][...]
-    squares = products = None
-    for side, shards in ((0, own), (1, other)):
+def part_kernel(where_ref, *refs):
+    mixed, weights = refs[:5], refs[5:21]
+    held_ref, acc_ref, sems = refs[21:]
+    copies = [pltpu.make_async_copy(ref, held_ref.at[j], sems.at[j]) for j, ref in enumerate(weights)]
+    for copy in copies:
+        copy.start()
+    for side in range(2):
+        for copy in copies[8 * side : 8 * side + 8]:
+            copy.wait()
         for tile in range(0, 512, 256):
             acc = None
-            for j in range(8):
-                part = jnp.dot(table[where_ref[8 + j]], shards[j][:, tile : tile + 256], preferred_element_type=F32)
+            for j in range(5):
+                block = held_ref[8 * side + where_ref[j], :, tile : tile + 256]
+                part = jnp.dot(mixed[j][...], block, preferred_element_type=F32)
                 acc = part if acc is None else acc + part
-            first = core if side == 0 else 1 - core
+            acc_ref[:, 512 * side + tile : 512 * side + tile + 256] = acc
+
+
+def partial_out(where, mixed, weights):
+    rows = mixed[0].shape[0]
+    return pl.pallas_call(
+        part_kernel,
+        in_specs=[SM] + [VM] * 5 + [pl.BlockSpec(memory_space=pl.ANY)] * 16,
+        out_specs=(VM, VM),
+        out_shape=(jax.ShapeDtypeStruct((16, 512, 512), BF), jax.ShapeDtypeStruct((rows, 1024), F32)),
+        scratch_shapes=[pltpu.SemaphoreType.DMA((16,))],
+        compiler_params=pltpu.CompilerParams(vmem_limit_bytes=20 * 2**20),
+        cost_estimate=pl.CostEstimate(flops=2 * 256 * 4096 * 1024, bytes_accessed=2**20, transcendentals=0),
+        name="part",
+    )(where, *mixed, *weights)
+
+
+def out_kernel(where_ref, *refs):
+    mixed, held_ref, acc_ref = refs[:3], refs[3], refs[4]
+    states_ref, gain_ref, head_ref, resid_ref, sums_ref = refs[5:]
+    core = where_ref[8]
+    squares = products = None
+    for side in range(2):
+        first = core if side == 0 else 1 - core
+        for tile in range(0, 512, 256):
+            acc = acc_ref[:, 512 * side + tile : 512 * side + tile + 256]
+            for j in range(3):
+                block = held_ref[8 * side + where_ref[5 + j], :, tile : tile + 256]
+                acc = acc + jnp.dot(mixed[j][...], block, preferred_element_type=F32)
             cols = pl.ds(pl.multiple_of(first * 512 + tile, 256), 256)
             resid = (states_ref[:, cols].astype(F32) + acc).astype(BF)
             resid_ref[:, cols] = resid
             stream = resid.astype(F32)
-            sq = jnp.sum(stream * stream, axis=1, keepdims=True)
-            pr = jnp.sum(stream * (gain_ref[:, cols] * head_ref[:, cols]), axis=1, keepdims=True)
+            sq = stream * stream
+            pr = stream * (gain_ref[:, cols] * head_ref[:, cols])
+            sq = sq[:, :128] + sq[:, 128:]
+            pr = pr[:, :128] + pr[:, 128:]
             squares = sq if squares is None else squares + sq
             products = pr if products is None else products + pr
-    lane = lax.broadcasted_iota(jnp.int32, (rows, 128), 1)
-    spread = jnp.where(lane == 0, squares, jnp.where(lane == 1, products, 0.0))
-    sums_ref[...] = jnp.transpose(spread)[:8]
-
-
-def finished(where, mixed, own, other, states, final_gain, head_weight):
+    sums_ref[0:1] = jnp.sum(jnp.transpose(squares), axis=0, keepdims=True)
+    sums_ref[1:2] = jnp.sum(jnp.transpose(products), axis=0, keepdims=True)
+
+
+def finished(where, mixed, held, acc, states, final_gain, head_weight):
     rows = states.shape[0]
     return pl.pallas_call(
         out_kernel,
-        in_specs=[SM] + [VM] * 27,
+        in_specs=[SM] + [VM] * 8,
         out_specs=(VM, VM),
-        out_shape=(jax.ShapeDtypeStruct((rows, 1024), BF), jax.ShapeDtypeStruct((8, rows), F32)),
-        scratch_shapes=[pltpu.VMEM((8, rows, 512), BF)],
-        compiler_params=pltpu.CompilerParams(vmem_limit_bytes=LIMIT // 2),
-        cost_estimate=pl.CostEstimate(flops=2 * 256 * 4096 * 1024, bytes_accessed=2**20, transcendentals=0),
+        out_shape=(jax.ShapeDtypeStruct((rows, 1024), BF), jax.ShapeDtypeStruct((2, rows), F32)),
+        compiler_params=pltpu.CompilerParams(vmem_limit_bytes=20 * 2**20),
+        cost_estimate=pl.CostEstimate(flops=2 * 256 * 1536 * 1024, bytes_accessed=2**20, transcendentals=0),
         name="finish",
-    )(where, *mixed, *own, *other, states, final_gain.reshape(1, 1024), head_weight.reshape(1, 1024))
+    )(where, *mixed, held, acc, states, final_gain.reshape(1, 1024), head_weight.reshape(1, 1024))
 
 
 def rope_tables(seg_row):
@@ -209,6 +238,9 @@
     angles = positions[:, None] * frequency[None, :]
     cosine, sine = jnp.cos(angles), jnp.sin(angles)
     return (jnp.concatenate([cosine, cosine], axis=1), jnp.concatenate([-sine, sine], axis=1))
+
+
+STAGES = (((0, 0), (0, 1), (0, 3), (1, 0)), ((0, 2), (1, 1), (1, 3)), ((1, 2),))
 
 
 def body(
@@ -250,17 +282,26 @@
     kb2 = shift(ka2, dy=1)
     qb2t, qb2b = shift(qa2t, dy=1), shift(qa2b, dy=1)
 
-    near = ((0, 0), (0, 1), (0, 3), (1, 0))
-    far = ((0, 2), (1, 1), (1, 3), (1, 2))
-    where = jnp.stack([chip(*p) for p in near])
-    acc = project(where, mine, got, [
-        [(0, w), (1, kv)], [(0, qa1), (1, ka1)], [(0, qa3), (1, ka3)], [(0, qb0), (1, kb0)]
-    ])
-    where = jnp.stack([chip(*p) for p in far])
-    own, other = project(where, mine, got, [
-        [(0, qa2t), (0, qa2b), (1, ka2)], [(0, qb1), (1, kb1)], [(0, qb3), (1, kb3)],
-        [(0, qb2t), (0, qb2b), (1, kb2)],
-    ], acc)
+    shards = {
+        (0, 0): [(0, w), (1, kv)],
+        (0, 1): [(0, qa1), (1, ka1)],
+        (0, 3): [(0, qa3), (1, ka3)],
+        (1, 0): [(0, qb0), (1, kb0)],
+        (0, 2): [(0, qa2t), (0, qa2b), (1, ka2)],
+        (1, 1): [(0, qb1), (1, kb1)],
+        (1, 3): [(0, qb3), (1, kb3)],
+        (1, 2): [(0, qb2t), (0, qb2b), (1, kb2)],
+    }
+    acc = None
+    for places in STAGES:
+        where = jnp.stack([chip(*p) for p in places])
+        rows_mine, rows_got = mine, got
+        if len(places) == 1:
+            rows_mine = lax.dynamic_slice_in_dim(mine, where[0], 1, 0)
+            rows_got = lax.dynamic_slice_in_dim(got, where[0], 1, 0)
+            where = jnp.zeros((1,), jnp.int32)
+        acc = project(where, rows_mine, rows_got, [shards[p] for p in places], acc)
+    own, other = acc
     back = shift(other, dc=1)
     cosine, sine = rope_tables(seg_row)
     mixed = attended(own, back, cosine, sine, seg_row)
@@ -269,7 +310,6 @@
     p0 = shift(out_block, dy=1)
     p1, p3, p2 = shift(p0, dz=1), shift(p0, dz=-1), shift(o2, dy=1)
     own_out = (out_block, o1, o3, o2, p0, p1, p3, p2)
-    out_places = ((0, 0), (0, 1), (0, 3), (0, 2), (1, 0), (1, 1), (1, 3), (1, 2))
     other_out = [shift(a, dc=1) for a in own_out]
 
     ml = shift(mixed, dl=1)
@@ -277,12 +317,16 @@
     mlx = [shift(ml, dx=k) for k in (1, 3, 2)]
     pieces = [mixed, ml, *mx, *mlx]
     peers = ((0, 0), (1, 0), (0, 1), (0, 3), (0, 2), (1, 1), (1, 3), (1, 2))
-    from_peer = [((y_lo + dl) % 2) * 4 + (x - k) % 4 for dl, k in peers]
-    where = jnp.stack(from_peer + [((y_hi + dy) % 2) * 4 + (z - k - x) % 4 for dy, k in out_places] + [core])
+    places = []
+    for dl, k in peers:
+        turn = (z - x - (x - k)) % 4
+        places.append(((y_lo + dl - y_hi) % 2) * 4 + (turn ^ (turn >> 1)))
+    where = jnp.stack(places + [core])
+    held, early = partial_out(where, pieces[:5], (*own_out, *other_out))
     cols = lax.dynamic_slice_in_dim(states, tensor * 1024, 1024, 1)
-    resid_out, sums = finished(where, pieces, own_out, other_out, cols, final_gain, head_weight)
+    resid_out, sums = finished(where, pieces[5:], held, early, cols, final_gain, head_weight)
     share = t_rows // 8
-    sums = jnp.transpose(sums[:2].reshape(2, 8, share), (1, 0, 2))
+    sums = jnp.transpose(sums.reshape(2, 8, share), (1, 0, 2))
     totals = lax.all_to_all(sums, "tensor", 0, 0, tiled=True).sum(axis=0)
     scores = totals[1] * lax.rsqrt(totals[0] / MODEL_WIDTH + EPS)
     return (scores, resid_out)

time: 185 us -> 183 us (0.989)
  waiting for transfers between devices: 52.1 us -> 36.4 us
  starting transfers between devices: 71.9 us -> 84.1 us
    ppermute x40, waiting for transfers between devices: 52.1 us -> 36.4 us  [shift(): return lax.ppermute(value, AXES, perm)]
    ppermute x40, starting transfers between devices: 68.8 us -> 81.9 us  [shift(): return lax.ppermute(value, AXES, perm)]
    pallas_call x1, Pallas kernels: 7.48 us -> 4.37 us  [normed_halves(): pl.pallas_call(norm_kernel, grid_spec=pltpu.PrefetchScalarGridSpec(num_sc...]
    pallas_call x2 -> x3, Pallas kernels: 7.01 us -> 9.4 us  [project(): pl.pallas_call(functools.partial(project_kernel, plan, acc is None), in_s...]
    pallas_call x1 -> x2, Pallas kernels: 5.81 us -> 7.58 us  [the longest x1 4.5 us: partial_out(): pl.pallas_call(part_kernel, in_specs=[SM] + [VM] * 5 + [pl.BlockSpec(memo...]
  transfers between devices with their start and end apart: 42 -> 42, of which waited for: 13 -> 10; matrix products, arithmetic and copies ran while one was open for 2% -> 3% of each run, Pallas kernels for 9% -> 9%
where the time goes in v1:
time: 183 us; the launch traced here: 182 us
  starting transfers between devices  84.1 us (46%)
  waiting for transfers between devices  36.4 us (20%)
  local copies, waits for them, and re-layouts  24.2 us (13%)
  Pallas kernels  24 us (13%)
  blocking collectives  9.86 us (5%)
  other arithmetic  2.58 us (1%)
    ppermute x40, starting transfers between devices, shift(): return lax.ppermute(value, AXES, perm)  81.9 us
    ppermute x40, waiting for transfers between devices, shift(): return lax.ppermute(value, AXES, perm)  36.4 us
    unnamed x77, local copies, waits for them, and re-layouts  20.9 us
    all_to_all x1, blocking collectives, body(): totals = lax.all_to_all(sums, 'tensor', 0, 0, tiled=True).sum(axis=0)  9.86 us
    pallas_call x3, Pallas kernels, project(): pl.pallas_call(functools.partial(project_kernel, plan, acc is None), in_s...  9.4 us
    pallas_call x1, Pallas kernels, partial_out(): pl.pallas_call(part_kernel, in_specs=[SM] + [VM] * 5 + [pl.BlockSpec(memo...  4.5 us
    pallas_call x1, Pallas kernels, normed_halves(): pl.pallas_call(norm_kernel, grid_spec=pltpu.PrefetchScalarGridSpec(num_sc...  4.37 us
  transfers between devices with their start and end apart: 42, of which 10 were waited for; matrix products, arithmetic and copies ran while one was open for 3% of the time, Pallas kernels for 9%

profile of v1, /device:TPU:0, one launch (start us, length us, event | category | flops | bytes accessed | tf_op | source)
XLA Modules:
  0.0 182.3 jit_solution(160259409506655746)
XLA Ops:
  0.7 2.2 %copy-done.26 = bf16[256,8192]{1,0:T(8,128)(2,1)S(1)} copy-done((bf16[256,8192]{1,0:T(8,128)(2,1)S(1)}, bf16[256,8192]{1,0:T(8,128)(2,1)}, u32[]{:S(2)}) %copy-start.26) | copy-done | bytes 4194328
  3.6 4.4 %norm.1 = (bf16[8,256,512]{2,1,0:T(8,128)(2,1)S(1)}, bf16[8,256,512]{2,1,0:T(8,128)(2,1)}) custom-call(s32[1]{0:T(128)} %bitcast.8.core_ref, bf16[256,8192]{1,0:T(8,128)(2,1)S(1)} %copy-done.26, f32[1,8192]{1,0:T(1,128)S(1)} %bitcast.36), custom_call_target="tpu_custom_call" | custom-call | flops 8000000000 | bytes 9437184 | tf_op jit(solution)/shard_map/norm/pallas_call | solution.py:58
  8.1 2.1 %collective-permute-start.11 = (bf16[512,256]{1,0:T(8,128)(2,1)S(1)}, bf16[512,256]{1,0:T(8,128)(2,1)S(1)}, u32[]{:S(2)}, u32[]{:S(2)}) collective-permute-start(bf16[512,256]{1,0:T(8,128)(2,1)S(1)} %constant_dynamic-update-slice_fusion.refs_3_), channel_id=1, source_target_pairs={{0,16},{1,17},{2,18},{3,19},{4,20},{5,21},{6,22},{7,23},{8,24},{9,... | collective-permute-start | bytes 786440 | tf_op jit(solution)/shard_map/ppermute | solution.py:33
  10.2 2.2 %collective-permute-start.14 = (bf16[512,256]{1,0:T(8,128)(2,1)S(1)}, bf16[512,256]{1,0:T(8,128)(2,1)S(1)}, u32[]{:S(2)}, u32[]{:S(2)}) collective-permute-start(bf16[512,256]{1,0:T(8,128)(2,1)S(1)} %constant_dynamic-update-slice_fusion.refs_3_), channel_id=1, source_target_pairs={{0,48},{1,49},{2,50},{3,51},{4,52},{5,53},{6,54},{7,55},{8,56},{9,... | collective-permute-start | bytes 786440 | tf_op jit(solution)/shard_map/ppermute | solution.py:33
  12.4 3.2 %collective-permute-start.16 = (bf16[512,256]{1,0:T(8,128)(2,1)S(1)}, bf16[512,256]{1,0:T(8,128)(2,1)S(1)}, u32[]{:S(2)}, u32[]{:S(2)}) collective-permute-start(bf16[512,256]{1,0:T(8,128)(2,1)S(1)} %constant_dynamic-update-slice_fusion.refs_3_), channel_id=1, source_target_pairs={{0,64},{1,65},{2,66},{3,67},{4,68},{5,69},{6,70},{7,71},{8,72},{9,... | collective-permute-start | bytes 786440 | tf_op jit(solution)/shard_map/ppermute | solution.py:33
  15.6 1.8 collective-permute-start.7
  17.3 1.9 %collective-permute-done.11.refs_5_ = bf16[512,256]{1,0:T(8,128)(2,1)S(1)} collective-permute-done((bf16[512,256]{1,0:T(8,128)(2,1)S(1)}, bf16[512,256]{1,0:T(8,128)(2,1)S(1)}, u32[]{:S(2)}, u32[]{:S(2)}) %collective-permute-start.11) | collective-permute-done | bytes 262176 | tf_op jit(solution)/shard_map/ppermute | solution.py:33
  19.3 3.2 %collective-permute-start.9 = (bf16[512,512]{1,0:T(8,128)(2,1)S(1)}, bf16[512,512]{1,0:T(8,128)(2,1)}, u32[]{:S(2)}, u32[]{:S(2)}) collective-permute-start(bf16[512,512]{1,0:T(8,128)(2,1)S(1)} %copy-done.8), channel_id=1, source_target_pairs={{0,64},{1,65},{2,66},{3,67},{4,68},{5,69},{6,70},{7,71},{8,72},{9,... | collective-permute-start | bytes 1572872 | tf_op jit(solution)/shard_map/ppermute | solution.py:33
  22.5 1.8 collective-permute-done.14.refs_7_
  24.3 3.0 %collective-permute-start.1 = (bf16[512,512]{1,0:T(8,128)(2,1)S(1)}, bf16[512,512]{1,0:T(8,128)(2,1)S(1)}, u32[]{:S(2)}, u32[]{:S(2)}) collective-permute-start(bf16[512,512]{1,0:T(8,128)(2,1)S(1)} %copy-done.8), channel_id=1, source_target_pairs={{0,16},{1,17},{2,18},{3,19},{4,20},{5,21},{6,22},{7,23},{8,24},{9,... | collective-permute-start | bytes 1572872 | tf_op jit(solution)/shard_map/ppermute | solution.py:33
  29.4 5.2 %collective-permute-done.9.refs_8_ = bf16[512,512]{1,0:T(8,128)(2,1)} collective-permute-done((bf16[512,512]{1,0:T(8,128)(2,1)S(1)}, bf16[512,512]{1,0:T(8,128)(2,1)}, u32[]{:S(2)}, u32[]{:S(2)}) %collective-permute-start.9) | collective-permute-done | bytes 524320 | tf_op jit(solution)/shard_map/ppermute | solution.py:33
  34.6 3.3 %collective-permute-start.12 = (bf16[512,256]{1,0:T(8,128)(2,1)S(1)}, bf16[512,256]{1,0:T(8,128)(2,1)S(1)}, u32[]{:S(2)}, u32[]{:S(2)}) collective-permute-start(bf16[512,256]{1,0:T(8,128)(2,1)S(1)} %collective-permute-done.11.refs_5_), channel_id=1, source_target_pairs={{0,64},{1,65},{2,66},{3,67},{4,68},{5,69},{6,70},{7,71},{8,72},{9,... | collective-permute-start | bytes 786440 | tf_op jit(solution)/shard_map/ppermute | solution.py:33
  37.9 1.8 %collective-permute-done.1.refs_4_ = bf16[512,512]{1,0:T(8,128)(2,1)S(1)} collective-permute-done((bf16[512,512]{1,0:T(8,128)(2,1)S(1)}, bf16[512,512]{1,0:T(8,128)(2,1)S(1)}, u32[]{:S(2)}, u32[]{:S(2)}) %collective-permute-start.1) | collective-permute-done | bytes 524320 | tf_op jit(solution)/shard_map/ppermute | solution.py:33
  39.8 3.1 %collective-permute-start.15 = (bf16[512,256]{1,0:T(8,128)(2,1)S(1)}, bf16[512,256]{1,0:T(8,128)(2,1)S(1)}, u32[]{:S(2)}, u32[]{:S(2)}) collective-permute-start(bf16[512,256]{1,0:T(8,128)(2,1)S(1)} %collective-permute-done.14.refs_7_), channel_id=1, source_target_pairs={{0,64},{1,65},{2,66},{3,67},{4,68},{5,69},{6,70},{7,71},{8,72},{9,... | collective-permute-start | bytes 786440 | tf_op jit(solution)/shard_map/ppermute | solution.py:33
  43.6 1.5 collective-permute-start.26
  45.1 16.7 %collective-permute-start.8 = (bf16[512,256]{1,0:T(8,128)(2,1)S(1)}, bf16[512,256]{1,0:T(8,128)(2,1)S(1)}, u32[]{:S(2)}, u32[]{:S(2)}) collective-permute-start(bf16[512,256]{1,0:T(8,128)(2,1)S(1)} %collective-permute-done.7.refs_4_), channel_id=1, source_target_pairs={{0,64},{1,65},{2,66},{3,67},{4,68},{5,69},{6,70},{7,71},{8,72},{9,... | collective-permute-start | bytes 786440 | tf_op jit(solution)/shard_map/ppermute | solution.py:33
  61.8 3.4 %collective-permute-start.2 = (bf16[256,512]{1,0:T(8,128)(2,1)S(1)}, bf16[256,512]{1,0:T(8,128)(2,1)}, u32[]{:S(2)}, u32[]{:S(2)}) collective-permute-start(bf16[256,512]{1,0:T(8,128)(2,1)S(1)} %slice.35), channel_id=1, source_target_pairs={{0,16},{1,17},{2,18},{3,19},{4,20},{5,21},{6,22},{7,23},{8,24},{9,... | collective-permute-start | bytes 786440 | tf_op jit(solution)/shard_map/ppermute | solution.py:33
  65.9 2.6 %collective-permute-start.5 = (bf16[256,512]{1,0:T(8,128)(2,1)S(1)}, bf16[256,512]{1,0:T(8,128)(2,1)}, u32[]{:S(2)}, u32[]{:S(2)}) collective-permute-start(bf16[256,512]{1,0:T(8,128)(2,1)S(1)} %slice.36), channel_id=1, source_target_pairs={{0,48},{1,49},{2,50},{3,51},{4,52},{5,53},{6,54},{7,55},{8,56},{9,... | collective-permute-start | bytes 786440 | tf_op jit(solution)/shard_map/ppermute | solution.py:33
  69.2 2.9 %collective-permute-start.10 = (bf16[512,512]{1,0:T(8,128)(2,1)}, bf16[512,512]{1,0:T(8,128)(2,1)}, u32[]{:S(2)}, u32[]{:S(2)}) collective-permute-start(bf16[512,512]{1,0:T(8,128)(2,1)} %collective-permute-done.9.refs_8_), channel_id=1, source_target_pairs={{0,16},{1,17},{2,18},{3,19},{4,20},{5,21},{6,22},{7,23},{8,24},{9,... | collective-permute-start | bytes 1572872 | tf_op jit(solution)/shard_map/ppermute | solution.py:33
  72.1 1.6 collective-permute-done.2.refs_2_
  73.7 1.7 collective-permute-start.13
  75.6 2.6 %collective-permute-start.3 = (bf16[256,512]{1,0:T(8,128)(2,1)}, bf16[256,512]{1,0:T(8,128)(2,1)}, u32[]{:S(2)}, u32[]{:S(2)}) collective-permute-start(bf16[256,512]{1,0:T(8,128)(2,1)} %collective-permute-done.2.refs_2_), channel_id=1, source_target_pairs={{0,64},{1,65},{2,66},{3,67},{4,68},{5,69},{6,70},{7,71},{8,72},{9,... | collective-permute-start | bytes 786440 | tf_op jit(solution)/shard_map/ppermute | solution.py:33
  78.2 1.0 collective-permute-start.30
  79.9 6.3 %collective-permute-done.10.refs_5_ = bf16[512,512]{1,0:T(8,128)(2,1)} collective-permute-done((bf16[512,512]{1,0:T(8,128)(2,1)}, bf16[512,512]{1,0:T(8,128)(2,1)}, u32[]{:S(2)}, u32[]{:S(2)}) %collective-permute-start.10) | collective-permute-done | bytes 524320 | tf_op jit(solution)/shard_map/ppermute | solution.py:33
  86.2 3.1 %collective-permute-start.6 = (bf16[256,512]{1,0:T(8,128)(2,1)}, bf16[256,512]{1,0:T(8,128)(2,1)S(1)}, u32[]{:S(2)}, u32[]{:S(2)}) collective-permute-start(bf16[256,512]{1,0:T(8,128)(2,1)} %collective-permute-done.5.refs_3_), channel_id=1, source_target_pairs={{0,64},{1,65},{2,66},{3,67},{4,68},{5,69},{6,70},{7,71},{8,72},{9,... | collective-permute-start | bytes 786440 | tf_op jit(solution)/shard_map/ppermute | solution.py:33
  89.3 1.6 collective-permute-start.29
  92.0 2.2 %collective-permute-start.28 = (bf16[512,512]{1,0:T(8,128)(2,1)}, bf16[512,512]{1,0:T(8,128)(2,1)}, u32[]{:S(2)}, u32[]{:S(2)}) collective-permute-start(bf16[512,512]{1,0:T(8,128)(2,1)} %collective-permute-done.26.refs_5_), channel_id=1, source_target_pairs={{0,48},{1,49},{2,50},{3,51},{4,52},{5,53},{6,54},{7,55},{8,56},{9,... | collective-permute-start | bytes 1572872 | tf_op jit(solution)/shard_map/ppermute | solution.py:33
  94.2 1.0 copy-done.9
  98.1 3.5 %shard_map.104 = (f32[256,768]{1,0:T(8,128)S(1)}, f32[256,768]{1,0:T(8,128)S(1)}) custom-call(s32[4]{0:T(128)S(1)} %pad_add_fusion.1.where_ref, bf16[8,256,512]{2,1,0:T(8,128)(2,1)S(1)} %get-tuple-element.14.refs_0_, bf16[8,256,512]{2,1,0:T(8,128)(2,1)} %collective-permute-done.refs_1_, bf16[512,512]{1,0:T(8,128)(2,1)S(1)} %copy-done.9, ...), custom_call_target="tpu_custom_call" | custom-call | flops 1610612736 | bytes 1048576 | tf_op jit(solution)/shard_map/pallas_call | solution.py:114
  102.9 3.4 %shard_map.105 = (f32[256,768]{1,0:T(8,128)S(1)}, f32[256,768]{1,0:T(8,128)S(1)}) custom-call(s32[3]{0:T(128)S(1)} %pad_add_fusion.where_ref, bf16[8,256,512]{2,1,0:T(8,128)(2,1)S(1)} %get-tuple-element.14.refs_0_, bf16[8,256,512]{2,1,0:T(8,128)(2,1)} %collective-permute-done.refs_1_, bf16[256,512]{1,0:T(8,128)(2,1)} %collective-permute-done.2.refs_2_, ...), custom_call_target="tpu_custom_call" | custom-call | flops 1610612736 | bytes 1048576 | tf_op jit(solution)/shard_map/pallas_call | solution.py:114
  106.3 3.3 %collective-permute-start.32 = (bf16[512,512]{1,0:T(8,128)(2,1)}, bf16[512,512]{1,0:T(8,128)(2,1)S(1)}, u32[]{:S(2)}, u32[]{:S(2)}) collective-permute-start(bf16[512,512]{1,0:T(8,128)(2,1)} %collective-permute-done.30.refs_9_), channel_id=1, source_target_pairs={{0,48},{1,49},{2,50},{3,51},{4,52},{5,53},{6,54},{7,55},{8,56},{9,... | collective-permute-start | bytes 1572872 | tf_op jit(solution)/shard_map/ppermute | solution.py:33
  109.6 5.1 %collective-permute-done.27.refs_6_ = bf16[512,512]{1,0:T(8,128)(2,1)} collective-permute-done((bf16[512,512]{1,0:T(8,128)(2,1)}, bf16[512,512]{1,0:T(8,128)(2,1)}, u32[]{:S(2)}, u32[]{:S(2)}) %collective-permute-start.27) | collective-permute-done | bytes 524320 | tf_op jit(solution)/shard_map/ppermute | solution.py:33
  114.7 1.4 collective-permute-start.33
  116.1 2.4 %shard_map.106 = (f32[256,768]{1,0:T(8,128)S(1)}, f32[256,768]{1,0:T(8,128)}) custom-call(s32[1]{0:T(128)} %constant.180.clone.1.where_ref, bf16[1,256,512]{2,1,0:T(8,128)(2,1)S(1)} %constant_dynamic-slice_fusion.2.refs_0_, bf16[1,256,512]{2,1,0:T(8,128)(2,1)S(1)} %constant_dynamic-slice_fusion.1.refs_1_, bf16[256,512]{1,0:T(8,128)(2,1)} %collective-permute-done.3.refs_2_, ...), custom_call_target="tpu_custom_call" | custom-call | flops 1610612736 | bytes 1048576 | tf_op jit(solution)/shard_map/pallas_call | solution.py:114
  120.2 5.3 %collective-permute-done.31.refs_10_ = bf16[512,512]{1,0:T(8,128)(2,1)S(1)} collective-permute-done((bf16[512,512]{1,0:T(8,128)(2,1)}, bf16[512,512]{1,0:T(8,128)(2,1)S(1)}, u32[]{:S(2)}, u32[]{:S(2)}) %collective-permute-start.31) | collective-permute-done | bytes 524320 | tf_op jit(solution)/shard_map/ppermute | solution.py:33
  126.1 3.6 %collective-permute-done.33.refs_12_ = bf16[512,512]{1,0:T(8,128)(2,1)S(1)} collective-permute-done((bf16[512,512]{1,0:T(8,128)(2,1)S(1)}, bf16[512,512]{1,0:T(8,128)(2,1)S(1)}, u32[]{:S(2)}, u32[]{:S(2)}) %collective-permute-start.33) | collective-permute-done | bytes 524320 | tf_op jit(solution)/shard_map/ppermute | solution.py:33
  136.2 1.1 copy-done.34
  137.4 2.7 %attend.1.refs_0_ = bf16[256,512]{1,0:T(8,128)(2,1)S(1)} custom-call(f32[256,768]{1,0:T(8,128)S(1)} %copy-done.34, f32[256,768]{1,0:T(8,128)} %collective-permute-done.17.b_ref, f32[256,128]{1,0:T(8,128)S(1)} %get-tuple-element.29.cos_ref, f32[256,128]{1,0:T(8,128)S(1)} %copy-done.24, s32[1,256]{1,0:T(1,128)S(1)} %copy-done.27, s32[256,1]{1,0:T(8,128)S(1)} %copy-done.25), custom_call_target="tpu_custom_call" | custom-call | flops 4000000000 | bytes 1048576 | tf_op jit(solution)/shard_map/attend/pallas_call | solution.py:148
  140.9 3.2 %collective-permute-start.23 = (bf16[256,512]{1,0:T(8,128)(2,1)S(1)}, bf16[256,512]{1,0:T(8,128)(2,1)}, u32[]{:S(2)}, u32[]{:S(2)}) collective-permute-start(bf16[256,512]{1,0:T(8,128)(2,1)S(1)} %attend.1.refs_0_), channel_id=1, source_target_pairs={{0,3},{1,0},{2,1},{3,2},{4,7},{5,4},{6,5},{7,6},{8,11},{9,8},{10,9... | collective-permute-start | bytes 786440 | tf_op jit(solution)/shard_map/ppermute | solution.py:33
  144.1 1.4 collective-permute-start.24
  145.5 3.6 %collective-permute-done.18.refs_1_ = bf16[256,512]{1,0:T(8,128)(2,1)} collective-permute-done((bf16[256,512]{1,0:T(8,128)(2,1)S(1)}, bf16[256,512]{1,0:T(8,128)(2,1)}, u32[]{:S(2)}, u32[]{:S(2)}) %collective-permute-start.18) | collective-permute-done | bytes 262176 | tf_op jit(solution)/shard_map/ppermute | solution.py:33
  149.2 3.2 %collective-permute-start.20 = (bf16[256,512]{1,0:T(8,128)(2,1)}, bf16[256,512]{1,0:T(8,128)(2,1)}, u32[]{:S(2)}, u32[]{:S(2)}) collective-permute-start(bf16[256,512]{1,0:T(8,128)(2,1)} %collective-permute-done.18.refs_1_), channel_id=1, source_target_pairs={{0,3},{1,0},{2,1},{3,2},{4,7},{5,4},{6,5},{7,6},{8,11},{9,8},{10,9... | collective-permute-start | bytes 786440 | tf_op jit(solution)/shard_map/ppermute | solution.py:33
  153.1 5.7 %collective-permute-start.21 = (bf16[256,512]{1,0:T(8,128)(2,1)}, bf16[256,512]{1,0:T(8,128)(2,1)}, u32[]{:S(2)}, u32[]{:S(2)}) collective-permute-start(bf16[256,512]{1,0:T(8,128)(2,1)} %collective-permute-done.18.refs_1_), channel_id=1, source_target_pairs={{0,2},{1,3},{2,0},{3,1},{4,6},{5,7},{6,4},{7,5},{8,10},{9,11},{10,... | collective-permute-start | bytes 786440 | tf_op jit(solution)/shard_map/ppermute | solution.py:33
  158.8 1.1 constant_dynamic-slice_fusion.refs_5_
  162.2 1.0 copy-done.7
  164.2 4.5 %part.1 = (bf16[16,512,512]{2,1,0:T(8,128)(2,1)S(1)}, f32[256,1024]{1,0:T(8,128)S(1)}) custom-call(s32[9]{0:T(128)S(1)} %stack.66.where_ref, bf16[256,512]{1,0:T(8,128)(2,1)S(1)} %attend.1.refs_0_, bf16[256,512]{1,0:T(8,128)(2,1)} %collective-permute-done.18.refs_1_, bf16[256,512]{1,0:T(8,128)(2,1)S(1)} %copy-done.17, ...), custom_call_target="tpu_custom_call" | custom-call | flops 2147483648 | bytes 1048576 | tf_op jit(solution)/shard_map/part/pallas_call | solution.py:179
  168.8 3.1 %finish.1 = (bf16[256,1024]{1,0:T(8,128)(2,1)}, f32[2,256]{1,0:T(2,128)S(1)}) custom-call(s32[9]{0:T(128)S(1)} %stack.66.where_ref, bf16[256,512]{1,0:T(8,128)(2,1)} %collective-permute-done.19.refs_0_, bf16[256,512]{1,0:T(8,128)(2,1)} %collective-permute-done.20.refs_1_, bf16[256,512]{1,0:T(8,128)(2,1)} %collective-permute-done.21.refs_2_, ...), custom_call_target="tpu_custom_call" | custom-call | flops 805306368 | bytes 1048576 | tf_op jit(solution)/shard_map/finish/pallas_call | solution.py:219
  171.9 9.9 %all_to_all.5 = f32[8,2,32]{2,1,0:T(2,128)S(1)} all-to-all(f32[8,2,32]{2,1,0:T(2,128)S(1)} %bitcast.37), channel_id=1, replica_groups=mesh['fsdp'=16,'tensor'=8] {'tensor'}, dimensions={0} | all-to-all | bytes 4096 | tf_op jit(solution)/shard_map/all_to_all | solution.py:330
  (145 shorter events, 25.1 us)
Async XLA Ops:
  3.6 24.4 %copy-start.37 = (bf16[512,512]{1,0:T(8,128)(2,1)S(1)}, bf16[512,512]{1,0:T(8,128)(2,1)}, u32[]{:S(2)}) copy-start(bf16[512,512]{1,0:T(8,128)(2,1)} %param.15) | copy-start | bytes 1572868
  3.6 71.9 %copy-start.27 = (s32[1,256]{1,0:T(1,128)S(1)}, s32[1,256]{1,0:T(1,128)}, u32[]{:S(2)}) copy-start(s32[1,256]{1,0:T(1,128)} %row_ref.1) | copy-start | bytes 3076
  8.0 84.0 %collective-permute-start = (bf16[8,256,512]{2,1,0:T(8,128)(2,1)}, bf16[8,256,512]{2,1,0:T(8,128)(2,1)}, u32[]{:S(2)}, u32[]{:S(2)}) collective-permute-start(bf16[8,256,512]{2,1,0:T(8,128)(2,1)} %get-tuple-element.15), channel_id=1, source_target_pairs={{0,8},{1,9},{2,10},{3,11},{4,12},{5,13},{6,14},{7,15},{8,0},{9,1},... | collective-permute-start | bytes 6291464 | tf_op jit(solution)/shard_map/ppermute | solution.py:33
  8.1 11.2 %collective-permute-start.11 = (bf16[512,256]{1,0:T(8,128)(2,1)S(1)}, bf16[512,256]{1,0:T(8,128)(2,1)S(1)}, u32[]{:S(2)}, u32[]{:S(2)}) collective-permute-start(bf16[512,256]{1,0:T(8,128)(2,1)S(1)} %constant_dynamic-update-slice_fusion.refs_3_), channel_id=1, source_target_pairs={{0,16},{1,17},{2,18},{3,19},{4,20},{5,21},{6,22},{7,23},{8,24},{9,... | collective-permute-start | bytes 786440 | tf_op jit(solution)/shard_map/ppermute | solution.py:33
  10.2 14.1 %collective-permute-start.14 = (bf16[512,256]{1,0:T(8,128)(2,1)S(1)}, bf16[512,256]{1,0:T(8,128)(2,1)S(1)}, u32[]{:S(2)}, u32[]{:S(2)}) collective-permute-start(bf16[512,256]{1,0:T(8,128)(2,1)S(1)} %constant_dynamic-update-slice_fusion.refs_3_), channel_id=1, source_target_pairs={{0,48},{1,49},{2,50},{3,51},{4,52},{5,53},{6,54},{7,55},{8,56},{9,... | collective-permute-start | bytes 786440 | tf_op jit(solution)/shard_map/ppermute | solution.py:33
  12.4 14.9 %collective-permute-start.16 = (bf16[512,256]{1,0:T(8,128)(2,1)S(1)}, bf16[512,256]{1,0:T(8,128)(2,1)S(1)}, u32[]{:S(2)}, u32[]{:S(2)}) collective-permute-start(bf16[512,256]{1,0:T(8,128)(2,1)S(1)} %constant_dynamic-update-slice_fusion.refs_3_), channel_id=1, source_target_pairs={{0,64},{1,65},{2,66},{3,67},{4,68},{5,69},{6,70},{7,71},{8,72},{9,... | collective-permute-start | bytes 786440 | tf_op jit(solution)/shard_map/ppermute | solution.py:33
  15.6 13.1 %collective-permute-start.7 = (bf16[512,256]{1,0:T(8,128)(2,1)S(1)}, bf16[512,256]{1,0:T(8,128)(2,1)S(1)}, u32[]{:S(2)}, u32[]{:S(2)}) collective-permute-start(bf16[512,256]{1,0:T(8,128)(2,1)S(1)} %constant_dynamic-update-slice_fusion.refs_3_), channel_id=1, source_target_pairs={{0,32},{1,33},{2,34},{3,35},{4,36},{5,37},{6,38},{7,39},{8,40},{9,... | collective-permute-start | bytes 786440 | tf_op jit(solution)/shard_map/ppermute | solution.py:33
  19.3 52.9 %copy-start.18 = (bf16[512,256]{1,0:T(8,128)(2,1)}, bf16[512,256]{1,0:T(8,128)(2,1)S(1)}, u32[]{:S(2)}) copy-start(bf16[512,256]{1,0:T(8,128)(2,1)S(1)} %collective-permute-done.11.refs_5_) | copy-start | bytes 786436
  19.3 15.4 %collective-permute-start.9 = (bf16[512,512]{1,0:T(8,128)(2,1)S(1)}, bf16[512,512]{1,0:T(8,128)(2,1)}, u32[]{:S(2)}, u32[]{:S(2)}) collective-permute-start(bf16[512,512]{1,0:T(8,128)(2,1)S(1)} %copy-done.8), channel_id=1, source_target_pairs={{0,64},{1,65},{2,66},{3,67},{4,68},{5,69},{6,70},{7,71},{8,72},{9,... | collective-permute-start | bytes 1572872 | tf_op jit(solution)/shard_map/ppermute | solution.py:33
  24.3 15.5 %collective-permute-start.1 = (bf16[512,512]{1,0:T(8,128)(2,1)S(1)}, bf16[512,512]{1,0:T(8,128)(2,1)S(1)}, u32[]{:S(2)}, u32[]{:S(2)}) collective-permute-start(bf16[512,512]{1,0:T(8,128)(2,1)S(1)} %copy-done.8), channel_id=1, source_target_pairs={{0,16},{1,17},{2,18},{3,19},{4,20},{5,21},{6,22},{7,23},{8,24},{9,... | collective-permute-start | bytes 1572872 | tf_op jit(solution)/shard_map/ppermute | solution.py:33
  28.0 15.6 %collective-permute-start.25 = (bf16[512,512]{1,0:T(8,128)(2,1)S(1)}, bf16[512,512]{1,0:T(8,128)(2,1)S(1)}, u32[]{:S(2)}, u32[]{:S(2)}) collective-permute-start(bf16[512,512]{1,0:T(8,128)(2,1)S(1)} %copy-done.37), channel_id=1, source_target_pairs={{0,0},{1,17},{2,34},{3,51},{4,64},{5,81},{6,98},{7,115},{8,8},{9,2... | collective-permute-start | bytes 1572872 | tf_op jit(solution)/shard_map/ppermute | solution.py:37
  28.7 16.4 %copy-start.10 = (bf16[512,256]{1,0:T(8,128)(2,1)}, bf16[512,256]{1,0:T(8,128)(2,1)S(1)}, u32[]{:S(2)}) copy-start(bf16[512,256]{1,0:T(8,128)(2,1)S(1)} %collective-permute-done.7.refs_4_) | copy-start | bytes 786436
  28.7 16.3 %collective-permute-start.4 = (bf16[512,512]{1,0:T(8,128)(2,1)S(1)}, bf16[512,512]{1,0:T(8,128)(2,1)S(1)}, u32[]{:S(2)}, u32[]{:S(2)}) collective-permute-start(bf16[512,512]{1,0:T(8,128)(2,1)S(1)} %copy-done.8), channel_id=1, source_target_pairs={{0,48},{1,49},{2,50},{3,51},{4,52},{5,53},{6,54},{7,55},{8,56},{9,... | collective-permute-start | bytes 1572872 | tf_op jit(solution)/shard_map/ppermute | solution.py:33
  34.6 27.2 %collective-permute-start.12 = (bf16[512,256]{1,0:T(8,128)(2,1)S(1)}, bf16[512,256]{1,0:T(8,128)(2,1)S(1)}, u32[]{:S(2)}, u32[]{:S(2)}) collective-permute-start(bf16[512,256]{1,0:T(8,128)(2,1)S(1)} %collective-permute-done.11.refs_5_), channel_id=1, source_target_pairs={{0,64},{1,65},{2,66},{3,67},{4,68},{5,69},{6,70},{7,71},{8,72},{9,... | collective-permute-start | bytes 786440 | tf_op jit(solution)/shard_map/ppermute | solution.py:33
  39.8 25.5 %collective-permute-start.15 = (bf16[512,256]{1,0:T(8,128)(2,1)S(1)}, bf16[512,256]{1,0:T(8,128)(2,1)S(1)}, u32[]{:S(2)}, u32[]{:S(2)}) collective-permute-start(bf16[512,256]{1,0:T(8,128)(2,1)S(1)} %collective-permute-done.14.refs_7_), channel_id=1, source_target_pairs={{0,64},{1,65},{2,66},{3,67},{4,68},{5,69},{6,70},{7,71},{8,72},{9,... | collective-permute-start | bytes 786440 | tf_op jit(solution)/shard_map/ppermute | solution.py:33
  43.6 34.6 %collective-permute-start.26 = (bf16[512,512]{1,0:T(8,128)(2,1)S(1)}, bf16[512,512]{1,0:T(8,128)(2,1)}, u32[]{:S(2)}, u32[]{:S(2)}) collective-permute-start(bf16[512,512]{1,0:T(8,128)(2,1)S(1)} %collective-permute-done.25), channel_id=1, source_target_pairs={{0,0},{1,3},{2,2},{3,1},{4,4},{5,7},{6,6},{7,5},{8,8},{9,11},{10,1... | collective-permute-start | bytes 1572872 | tf_op jit(solution)/shard_map/ppermute | solution.py:37
  45.1 23.4 %collective-permute-start.8 = (bf16[512,256]{1,0:T(8,128)(2,1)S(1)}, bf16[512,256]{1,0:T(8,128)(2,1)S(1)}, u32[]{:S(2)}, u32[]{:S(2)}) collective-permute-start(bf16[512,256]{1,0:T(8,128)(2,1)S(1)} %collective-permute-done.7.refs_4_), channel_id=1, source_target_pairs={{0,64},{1,65},{2,66},{3,67},{4,68},{5,69},{6,70},{7,71},{8,72},{9,... | collective-permute-start | bytes 786440 | tf_op jit(solution)/shard_map/ppermute | solution.py:33
  61.8 12.0 %collective-permute-start.2 = (bf16[256,512]{1,0:T(8,128)(2,1)S(1)}, bf16[256,512]{1,0:T(8,128)(2,1)}, u32[]{:S(2)}, u32[]{:S(2)}) collective-permute-start(bf16[256,512]{1,0:T(8,128)(2,1)S(1)} %slice.35), channel_id=1, source_target_pairs={{0,16},{1,17},{2,18},{3,19},{4,20},{5,21},{6,22},{7,23},{8,24},{9,... | collective-permute-start | bytes 786440 | tf_op jit(solution)/shard_map/ppermute | solution.py:33
  65.9 9.7 %collective-permute-start.5 = (bf16[256,512]{1,0:T(8,128)(2,1)S(1)}, bf16[256,512]{1,0:T(8,128)(2,1)}, u32[]{:S(2)}, u32[]{:S(2)}) collective-permute-start(bf16[256,512]{1,0:T(8,128)(2,1)S(1)} %slice.36), channel_id=1, source_target_pairs={{0,48},{1,49},{2,50},{3,51},{4,52},{5,53},{6,54},{7,55},{8,56},{9,... | collective-permute-start | bytes 786440 | tf_op jit(solution)/shard_map/ppermute | solution.py:33
  69.2 17.0 %collective-permute-start.10 = (bf16[512,512]{1,0:T(8,128)(2,1)}, bf16[512,512]{1,0:T(8,128)(2,1)}, u32[]{:S(2)}, u32[]{:S(2)}) collective-permute-start(bf16[512,512]{1,0:T(8,128)(2,1)} %collective-permute-done.9.refs_8_), channel_id=1, source_target_pairs={{0,16},{1,17},{2,18},{3,19},{4,20},{5,21},{6,22},{7,23},{8,24},{9,... | collective-permute-start | bytes 1572872 | tf_op jit(solution)/shard_map/ppermute | solution.py:33
  73.7 15.5 %collective-permute-start.13 = (bf16[512,512]{1,0:T(8,128)(2,1)}, bf16[512,512]{1,0:T(8,128)(2,1)}, u32[]{:S(2)}, u32[]{:S(2)}) collective-permute-start(bf16[512,512]{1,0:T(8,128)(2,1)} %collective-permute-done.9.refs_8_), channel_id=1, source_target_pairs={{0,48},{1,49},{2,50},{3,51},{4,52},{5,53},{6,54},{7,55},{8,56},{9,... | collective-permute-start | bytes 1572872 | tf_op jit(solution)/shard_map/ppermute | solution.py:33
  75.6 15.3 %collective-permute-start.3 = (bf16[256,512]{1,0:T(8,128)(2,1)}, bf16[256,512]{1,0:T(8,128)(2,1)}, u32[]{:S(2)}, u32[]{:S(2)}) collective-permute-start(bf16[256,512]{1,0:T(8,128)(2,1)} %collective-permute-done.2.refs_2_), channel_id=1, source_target_pairs={{0,64},{1,65},{2,66},{3,67},{4,68},{5,69},{6,70},{7,71},{8,72},{9,... | collective-permute-start | bytes 786440 | tf_op jit(solution)/shard_map/ppermute | solution.py:33
  78.2 23.6 %collective-permute-start.30 = (bf16[512,512]{1,0:T(8,128)(2,1)}, bf16[512,512]{1,0:T(8,128)(2,1)}, u32[]{:S(2)}, u32[]{:S(2)}) collective-permute-start(bf16[512,512]{1,0:T(8,128)(2,1)} %collective-permute-done.26.refs_5_), channel_id=1, source_target_pairs={{0,64},{1,65},{2,66},{3,67},{4,68},{5,69},{6,70},{7,71},{8,72},{9,... | collective-permute-start | bytes 1572872 | tf_op jit(solution)/shard_map/ppermute | solution.py:33
  86.2 15.4 %collective-permute-start.6 = (bf16[256,512]{1,0:T(8,128)(2,1)}, bf16[256,512]{1,0:T(8,128)(2,1)S(1)}, u32[]{:S(2)}, u32[]{:S(2)}) collective-permute-start(bf16[256,512]{1,0:T(8,128)(2,1)} %collective-permute-done.5.refs_3_), channel_id=1, source_target_pairs={{0,64},{1,65},{2,66},{3,67},{4,68},{5,69},{6,70},{7,71},{8,72},{9,... | collective-permute-start | bytes 786440 | tf_op jit(solution)/shard_map/ppermute | solution.py:33
  89.3 17.0 %collective-permute-start.29 = (bf16[512,512]{1,0:T(8,128)(2,1)}, bf16[512,512]{1,0:T(8,128)(2,1)S(1)}, u32[]{:S(2)}, u32[]{:S(2)}) collective-permute-start(bf16[512,512]{1,0:T(8,128)(2,1)} %collective-permute-done.26.refs_5_), channel_id=1, source_target_pairs={{0,32},{1,33},{2,34},{3,35},{4,36},{5,37},{6,38},{7,39},{8,40},{9,... | collective-permute-start | bytes 1572872 | tf_op jit(solution)/shard_map/ppermute | solution.py:33
  90.9 23.9 %collective-permute-start.27 = (bf16[512,512]{1,0:T(8,128)(2,1)}, bf16[512,512]{1,0:T(8,128)(2,1)}, u32[]{:S(2)}, u32[]{:S(2)}) collective-permute-start(bf16[512,512]{1,0:T(8,128)(2,1)} %collective-permute-done.26.refs_5_), channel_id=1, source_target_pairs={{0,16},{1,17},{2,18},{3,19},{4,20},{5,21},{6,22},{7,23},{8,24},{9,... | collective-permute-start | bytes 1572872 | tf_op jit(solution)/shard_map/ppermute | solution.py:33
  92.0 27.5 %collective-permute-start.28 = (bf16[512,512]{1,0:T(8,128)(2,1)}, bf16[512,512]{1,0:T(8,128)(2,1)}, u32[]{:S(2)}, u32[]{:S(2)}) collective-permute-start(bf16[512,512]{1,0:T(8,128)(2,1)} %collective-permute-done.26.refs_5_), channel_id=1, source_target_pairs={{0,48},{1,49},{2,50},{3,51},{4,52},{5,53},{6,54},{7,55},{8,56},{9,... | collective-permute-start | bytes 1572872 | tf_op jit(solution)/shard_map/ppermute | solution.py:33
  101.7 17.9 %collective-permute-start.34 = (bf16[512,512]{1,0:T(8,128)(2,1)}, bf16[512,512]{1,0:T(8,128)(2,1)S(1)}, u32[]{:S(2)}, u32[]{:S(2)}) collective-permute-start(bf16[512,512]{1,0:T(8,128)(2,1)} %collective-permute-done.26.refs_5_), channel_id=1, source_target_pairs={{0,8},{1,9},{2,10},{3,11},{4,12},{5,13},{6,14},{7,15},{8,0},{9,1},... | collective-permute-start | bytes 1572872 | tf_op jit(solution)/shard_map/ppermute | solution.py:33
  101.8 23.7 %collective-permute-start.31 = (bf16[512,512]{1,0:T(8,128)(2,1)}, bf16[512,512]{1,0:T(8,128)(2,1)S(1)}, u32[]{:S(2)}, u32[]{:S(2)}) collective-permute-start(bf16[512,512]{1,0:T(8,128)(2,1)} %collective-permute-done.30.refs_9_), channel_id=1, source_target_pairs={{0,16},{1,17},{2,18},{3,19},{4,20},{5,21},{6,22},{7,23},{8,24},{9,... | collective-permute-start | bytes 1572872 | tf_op jit(solution)/shard_map/ppermute | solution.py:33
  106.3 19.1 %copy-start = (bf16[512,512]{1,0:T(8,128)(2,1)}, bf16[512,512]{1,0:T(8,128)(2,1)S(1)}, u32[]{:S(2)}) copy-start(bf16[512,512]{1,0:T(8,128)(2,1)S(1)} %collective-permute-done.29.refs_8_) | copy-start | bytes 1572868
  106.3 19.2 %collective-permute-start.32 = (bf16[512,512]{1,0:T(8,128)(2,1)}, bf16[512,512]{1,0:T(8,128)(2,1)S(1)}, u32[]{:S(2)}, u32[]{:S(2)}) collective-permute-start(bf16[512,512]{1,0:T(8,128)(2,1)} %collective-permute-done.30.refs_9_), channel_id=1, source_target_pairs={{0,48},{1,49},{2,50},{3,51},{4,52},{5,53},{6,54},{7,55},{8,56},{9,... | collective-permute-start | bytes 1572872 | tf_op jit(solution)/shard_map/ppermute | solution.py:33
  114.7 14.9 %collective-permute-start.33 = (bf16[512,512]{1,0:T(8,128)(2,1)S(1)}, bf16[512,512]{1,0:T(8,128)(2,1)S(1)}, u32[]{:S(2)}, u32[]{:S(2)}) collective-permute-start(bf16[512,512]{1,0:T(8,128)(2,1)S(1)} %collective-permute-done.29.refs_8_), channel_id=1, source_target_pairs={{0,64},{1,65},{2,66},{3,67},{4,68},{5,69},{6,70},{7,71},{8,72},{9,... | collective-permute-start | bytes 1572872 | tf_op jit(solution)/shard_map/ppermute | solution.py:33
  119.5 14.4 %collective-permute-start.17 = (f32[256,768]{1,0:T(8,128)}, f32[256,768]{1,0:T(8,128)}, u32[]{:S(2)}, u32[]{:S(2)}) collective-permute-start(f32[256,768]{1,0:T(8,128)} %get-tuple-element.21), channel_id=1, source_target_pairs={{0,8},{1,9},{2,10},{3,11},{4,12},{5,13},{6,14},{7,15},{8,0},{9,1},... | collective-permute-start | bytes 2359304 | tf_op jit(solution)/shard_map/ppermute | solution.py:33
  119.6 10.6 %collective-permute-start.38 = (bf16[512,512]{1,0:T(8,128)(2,1)}, bf16[512,512]{1,0:T(8,128)(2,1)S(1)}, u32[]{:S(2)}, u32[]{:S(2)}) collective-permute-start(bf16[512,512]{1,0:T(8,128)(2,1)} %collective-permute-done.30.refs_9_), channel_id=1, source_target_pairs={{0,8},{1,9},{2,10},{3,11},{4,12},{5,13},{6,14},{7,15},{8,0},{9,1},... | collective-permute-start | bytes 1572872 | tf_op jit(solution)/shard_map/ppermute | solution.py:33
  125.4 6.1 %collective-permute-start.37 = (bf16[512,512]{1,0:T(8,128)(2,1)S(1)}, bf16[512,512]{1,0:T(8,128)(2,1)S(1)}, u32[]{:S(2)}, u32[]{:S(2)}) collective-permute-start(bf16[512,512]{1,0:T(8,128)(2,1)S(1)} %collective-permute-done.29.refs_8_), channel_id=1, source_target_pairs={{0,8},{1,9},{2,10},{3,11},{4,12},{5,13},{6,14},{7,15},{8,0},{9,1},... | collective-permute-start | bytes 1572872 | tf_op jit(solution)/shard_map/ppermute | solution.py:33
  125.5 14.5 %collective-permute-start.35 = (bf16[512,512]{1,0:T(8,128)(2,1)}, bf16[512,512]{1,0:T(8,128)(2,1)S(1)}, u32[]{:S(2)}, u32[]{:S(2)}) collective-permute-start(bf16[512,512]{1,0:T(8,128)(2,1)} %collective-permute-done.27.refs_6_), channel_id=1, source_target_pairs={{0,8},{1,9},{2,10},{3,11},{4,12},{5,13},{6,14},{7,15},{8,0},{9,1},... | collective-permute-start | bytes 1572872 | tf_op jit(solution)/shard_map/ppermute | solution.py:33
  129.7 11.2 %collective-permute-start.36 = (bf16[512,512]{1,0:T(8,128)(2,1)}, bf16[512,512]{1,0:T(8,128)(2,1)}, u32[]{:S(2)}, u32[]{:S(2)}) collective-permute-start(bf16[512,512]{1,0:T(8,128)(2,1)} %collective-permute-done.28.refs_7_), channel_id=1, source_target_pairs={{0,8},{1,9},{2,10},{3,11},{4,12},{5,13},{6,14},{7,15},{8,0},{9,1},... | collective-permute-start | bytes 1572872 | tf_op jit(solution)/shard_map/ppermute | solution.py:33
  131.0 9.9 %collective-permute-start.39 = (bf16[512,512]{1,0:T(8,128)(2,1)S(1)}, bf16[512,512]{1,0:T(8,128)(2,1)}, u32[]{:S(2)}, u32[]{:S(2)}) collective-permute-start(bf16[512,512]{1,0:T(8,128)(2,1)S(1)} %collective-permute-done.31.refs_10_), channel_id=1, source_target_pairs={{0,8},{1,9},{2,10},{3,11},{4,12},{5,13},{6,14},{7,15},{8,0},{9,1},... | collective-permute-start | bytes 1572872 | tf_op jit(solution)/shard_map/ppermute | solution.py:33
  132.3 11.7 %collective-permute-start.40 = (bf16[512,512]{1,0:T(8,128)(2,1)S(1)}, bf16[512,512]{1,0:T(8,128)(2,1)}, u32[]{:S(2)}, u32[]{:S(2)}) collective-permute-start(bf16[512,512]{1,0:T(8,128)(2,1)S(1)} %collective-permute-done.32.refs_11_), channel_id=1, source_target_pairs={{0,8},{1,9},{2,10},{3,11},{4,12},{5,13},{6,14},{7,15},{8,0},{9,1},... | collective-permute-start | bytes 1572872 | tf_op jit(solution)/shard_map/ppermute | solution.py:33
  133.9 15.3 %collective-permute-start.41 = (bf16[512,512]{1,0:T(8,128)(2,1)S(1)}, bf16[512,512]{1,0:T(8,128)(2,1)}, u32[]{:S(2)}, u32[]{:S(2)}) collective-permute-start(bf16[512,512]{1,0:T(8,128)(2,1)S(1)} %collective-permute-done.33.refs_12_), channel_id=1, source_target_pairs={{0,8},{1,9},{2,10},{3,11},{4,12},{5,13},{6,14},{7,15},{8,0},{9,1},... | collective-permute-start | bytes 1572872 | tf_op jit(solution)/shard_map/ppermute | solution.py:33
  137.4 22.8 %copy-start.1 = (bf16[512,512]{1,0:T(8,128)(2,1)S(1)}, bf16[512,512]{1,0:T(8,128)(2,1)}, u32[]{:S(2)}) copy-start(bf16[512,512]{1,0:T(8,128)(2,1)} %copy-done) | copy-start | bytes 1572868
  140.8 8.3 %collective-permute-start.18 = (bf16[256,512]{1,0:T(8,128)(2,1)S(1)}, bf16[256,512]{1,0:T(8,128)(2,1)}, u32[]{:S(2)}, u32[]{:S(2)}) collective-permute-start(bf16[256,512]{1,0:T(8,128)(2,1)S(1)} %attend.1.refs_0_), channel_id=1, source_target_pairs={{0,4},{1,5},{2,6},{3,7},{4,0},{5,1},{6,2},{7,3},{8,12},{9,13},{10,... | collective-permute-start | bytes 786440 | tf_op jit(solution)/shard_map/ppermute | solution.py:33
  140.8 11.6 %collective-permute-start.22 = (bf16[256,512]{1,0:T(8,128)(2,1)S(1)}, bf16[256,512]{1,0:T(8,128)(2,1)S(1)}, u32[]{:S(2)}, u32[]{:S(2)}) collective-permute-start(bf16[256,512]{1,0:T(8,128)(2,1)S(1)} %attend.1.refs_0_), channel_id=1, source_target_pairs={{0,1},{1,2},{2,3},{3,0},{4,5},{5,6},{6,7},{7,4},{8,9},{9,10},{10,1... | collective-permute-start | bytes 786440 | tf_op jit(solution)/shard_map/ppermute | solution.py:33
  140.9 19.2 %collective-permute-start.23 = (bf16[256,512]{1,0:T(8,128)(2,1)S(1)}, bf16[256,512]{1,0:T(8,128)(2,1)}, u32[]{:S(2)}, u32[]{:S(2)}) collective-permute-start(bf16[256,512]{1,0:T(8,128)(2,1)S(1)} %attend.1.refs_0_), channel_id=1, source_target_pairs={{0,3},{1,0},{2,1},{3,2},{4,7},{5,4},{6,5},{7,6},{8,11},{9,8},{10,9... | collective-permute-start | bytes 786440 | tf_op jit(solution)/shard_map/ppermute | solution.py:33
  144.1 16.0 %collective-permute-start.24 = (bf16[256,512]{1,0:T(8,128)(2,1)S(1)}, bf16[256,512]{1,0:T(8,128)(2,1)}, u32[]{:S(2)}, u32[]{:S(2)}) collective-permute-start(bf16[256,512]{1,0:T(8,128)(2,1)S(1)} %attend.1.refs_0_), channel_id=1, source_target_pairs={{0,2},{1,3},{2,0},{3,1},{4,6},{5,7},{6,4},{7,5},{8,10},{9,11},{10,... | collective-permute-start | bytes 786440 | tf_op jit(solution)/shard_map/ppermute | solution.py:33
  149.2 19.6 %collective-permute-start.19 = (bf16[256,512]{1,0:T(8,128)(2,1)}, bf16[256,512]{1,0:T(8,128)(2,1)}, u32[]{:S(2)}, u32[]{:S(2)}) collective-permute-start(bf16[256,512]{1,0:T(8,128)(2,1)} %collective-permute-done.18.refs_1_), channel_id=1, source_target_pairs={{0,1},{1,2},{2,3},{3,0},{4,5},{5,6},{6,7},{7,4},{8,9},{9,10},{10,1... | collective-permute-start | bytes 786440 | tf_op jit(solution)/shard_map/ppermute | solution.py:33
  149.2 19.6 %collective-permute-start.20 = (bf16[256,512]{1,0:T(8,128)(2,1)}, bf16[256,512]{1,0:T(8,128)(2,1)}, u32[]{:S(2)}, u32[]{:S(2)}) collective-permute-start(bf16[256,512]{1,0:T(8,128)(2,1)} %collective-permute-done.18.refs_1_), channel_id=1, source_target_pairs={{0,3},{1,0},{2,1},{3,2},{4,7},{5,4},{6,5},{7,6},{8,11},{9,8},{10,9... | collective-permute-start | bytes 786440 | tf_op jit(solution)/shard_map/ppermute | solution.py:33
  153.1 15.6 %collective-permute-start.21 = (bf16[256,512]{1,0:T(8,128)(2,1)}, bf16[256,512]{1,0:T(8,128)(2,1)}, u32[]{:S(2)}, u32[]{:S(2)}) collective-permute-start(bf16[256,512]{1,0:T(8,128)(2,1)} %collective-permute-done.18.refs_1_), channel_id=1, source_target_pairs={{0,2},{1,3},{2,0},{3,1},{4,6},{5,7},{6,4},{7,5},{8,10},{9,11},{10,... | collective-permute-start | bytes 786440 | tf_op jit(solution)/shard_map/ppermute | solution.py:33
  (32 other events, 92.8 us)
